TPU v7x, 256 devices: a whole 4x4x8 slice. The times are simulated.
256 devices in a mesh: dp: 16 (over x_hi, z), param: 16 (over y, x_lo, core).
Axes of the slice: x: 4 (x_hi: 2, x_lo: 2; x = x_hi * 2 + x_lo), y: 4, z: 8, core: 2. Of those that a mesh axis runs over, the one named last changes fastest.
Arguments:
- ex_grads: bfloat16 [1536, 20480], P('dp', 'param'), may hold values from -6 to 6
- tgt_grads: bfloat16 [4096, 20480], P('dp', 'param'), may hold values from -6 to 6
- projection: bfloat16 [20480, 4096], P('param'), may hold values from -0.0390625 to 0.0390625
- example_weight: float32 [1536], P('param'), may hold values from 0.05 to 1
Outputs:
- scores: float32 [4096, 1536], P('dp', 'param')
All inputs are finite; a program needn't handle non-finite values.
Results may differ from a plain program's by a relative error of at most 0.0078.
Values may be sent and summed in bfloat16 or wider, within the bound.
A program may use at most 192 MiB of HBM per device.

v0:
```python
import math

import jax
import jax.numpy as jnp
from jax import lax
from jax.sharding import PartitionSpec as P

ridge_value = 0.5


def sent_to_all(x, axis):
    length = lax.axis_size(axis)
    return lax.all_to_all(jnp.broadcast_to(x[None], (length, *x.shape)), axis, 0, 0, tiled=True)


def in_order(parts, dim):
    parts = jnp.moveaxis(parts, 0, dim)
    lengths = parts.shape
    return parts.reshape(*lengths[:dim], lengths[dim] * lengths[dim + 1], *lengths[dim + 2 :])


def gather_directly(x, axis, dim):
    parts = sent_to_all(x, axis)
    return in_order(parts, dim)


def with_ridge(block, first_row):
    row_ids = lax.broadcasted_iota(jnp.int32, block.shape, 0) + first_row
    col_ids = lax.broadcasted_iota(jnp.int32, block.shape, 1)
    return block + jnp.where(row_ids == col_ids, ridge_value, 0.0).astype(jnp.float32)


def on_device(ex_grads, tgt_grads, projection, example_weight):
    ex_rows = ex_grads.shape[0]
    columns = projection.shape[1]
    param_total = lax.axis_size("param")
    param_pos = lax.axis_index("param")
    replica_pos = lax.axis_index("dp")
    stacked = jnp.concatenate([ex_grads, tgt_grads], axis=0)
    contract_rows = (((0,), (1,)), ((), ()))
    feature_block = lax.psum_scatter(
        lax.dot_general(projection, stacked, contract_rows, preferred_element_type=jnp.float32),
        "param",
        scatter_dimension=0,
        tiled=True,
    )
    local_features = feature_block.astype(jnp.bfloat16)
    example_part = local_features[:, :ex_rows]
    contract_first = (((0,), (0,)), ((), ()))
    partial_value = lax.dot_general(
        local_features,
        gather_directly(example_part, "dp", 1),
        contract_first,
        preferred_element_type=jnp.float32,
    )
    examples = partial_value.shape[1]
    summed = lax.psum(partial_value, "param")
    kernel_block = with_ridge(summed[:ex_rows] / columns, replica_pos * ex_rows)
    kernel = lax.all_gather(kernel_block, "dp", axis=0, tiled=True)
    cross_terms = summed[ex_rows:] / columns
    factor = jnp.linalg.cholesky(kernel)
    forward = jax.scipy.linalg.solve_triangular(factor, cross_terms.T, lower=True)
    solved = jax.scipy.linalg.solve_triangular(factor, forward, lower=True, trans=1)
    block_cols = examples // param_total
    chosen = lax.dynamic_slice_in_dim(solved.T, param_pos * block_cols, block_cols, 1)
    return chosen * math.sqrt(columns) * example_weight[None, :]


def solution(mesh):
    placed = (P("dp", "param"), P("dp", "param"), P("param", None), P("param"))
    return jax.shard_map(
        on_device, mesh=mesh, in_specs=placed, out_specs=P("dp", "param"), check_vma=False
    )
```

profile of v0, /device:TPU:1, one launch (start us, length us, event | category | flops | bytes accessed | tf_op | source)
XLA Modules:
  0.0 965.1 jit_solution(2935307158991540555)
XLA Ops:
  6.5 10.7 %convolution_bitcast_fusion = f32[4096,352]{0,1:T(8,128)} fusion(bf16[1280,4096]{1,0:T(8,128)(2,1)} %param.6, bf16[256,1280]{1,0:T(8,128)(2,1)} %param.5, bf16[96,1280]{1,0:T(8,128)(2,1)} %param.4), kind=kOutput, calls=%fused_computation.6 | convolution fusion | flops 3692789760 | bytes 17154048 | tf_op jit(solution)/shard_map/dot_general | solution.py:42
  17.3 79.7 %reduce-scatter.2.cloned.1.call-done = f32[256,352]{0,1:T(8,128)} async-done(((f32[4096,352]{0,1:T(8,128)}), f32[256,352]{0,1:T(8,128)}) %reduce-scatter.2.cloned.1.call-update) | async-done | bytes 360464 | tf_op jit(solution)/shard_map/reduce_scatter | solution.py:41
  98.1 27.1 %all_to_all.5 = bf16[16,256,96]{1,2,0:T(8,128)(2,1)S(1)} all-to-all(bf16[16,256,96]{1,2,0:T(8,128)(2,1)S(1)} %broadcast_in_dim.17), channel_id=1, replica_groups=mesh['dp'=16,'param'=16] {'dp'}, dimensions={0} | all-to-all | bytes 1572864 | tf_op jit(solution)/shard_map/all_to_all | solution.py:13
  127.1 130.4 %all-reduce.3.cloned.1.call-done = f32[352,1536]{1,0:T(8,128)} async-done(((f32[352,1536]{1,0:T(8,128)}), f32[352,1536]{1,0:T(8,128)}) %all-reduce.3.cloned.1.call-update) | async-done | bytes 2162704 | tf_op jit(solution)/shard_map/psum | solution.py:57
  261.1 144.9 %all-gather.2.cloned.1.call-done = f32[1536,1536]{1,0:T(8,128)} async-done(((f32[96,1536]{1,0:T(8,128)}), f32[1536,1536]{1,0:T(8,128)}) %all-gather.2.cloned.1.call-update) | async-done | bytes 9437200 | tf_op jit(solution)/shard_map/all_gather | solution.py:59
  406.0 10.1 %copy.10 = f32[1536,1536]{0,1:T(8,128)} copy(f32[1536,1536]{1,0:T(8,128)} %all-gather.2.cloned.1.call-done) | data formatting | bytes 18874368 | tf_op jit(solution)/shard_map/all_gather | solution.py:59
  416.1 12.3 %fusion = f32[1536,1536]{1,0:T(8,128)} fusion(f32[1536,1536]{1,0:T(8,128)} %all-gather.2.cloned.1.call-done, f32[1536,1536]{0,1:T(8,128)} %copy.10), kind=kLoop, calls=%fused_computation.4 | loop fusion | flops 4718592 | bytes 28311552 | tf_op jit(solution)/shard_map/jit(cholesky)/div | solution.py:61
  429.3 11.7 %cholesky.341 = f32[128,128]{1,0:T(8,128)S(1)} custom-call(f32[128,128]{1,0:T(8,128)S(1)} %cholesky.892), custom_call_target="Cholesky" | custom-call | tf_op jit(solution)/shard_map/jit(cholesky)/cholesky | solution.py:61
  441.0 4.8 cholesky.371
  445.8 9.8 %custom-call.98 = f32[1,128,128]{1,2,0:T(8,128)S(1)} custom-call(f32[1,128,128]{2,1,0:T(8,128)S(1)} %get-tuple-element.111), custom_call_target="InvertDiagBlocksLowerTriangular" | custom-call | tf_op jit(solution)/shard_map/jit(cholesky)/cholesky | solution.py:61
  455.6 2.8 constant_dynamic-update-slice_fusion.134
  460.3 11.9 %cholesky.362 = f32[128,128]{1,0:T(8,128)S(1)} custom-call(f32[128,128]{1,0:T(8,128)S(1)} %cholesky.896), custom_call_target="Cholesky" | custom-call | tf_op jit(solution)/shard_map/jit(cholesky)/cholesky | solution.py:61
  472.9 9.8 %custom-call.99 = f32[1,128,128]{1,2,0:T(8,128)S(1)} custom-call(f32[1,128,128]{2,1,0:T(8,128)S(1)} %get-tuple-element.108), custom_call_target="InvertDiagBlocksLowerTriangular" | custom-call | tf_op jit(solution)/shard_map/jit(cholesky)/cholesky | solution.py:61
  484.2 2.8 convolution_subtract_fusion.1
  487.0 11.7 %cholesky.385 = f32[128,128]{1,0:T(8,128)S(1)} custom-call(f32[128,128]{1,0:T(8,128)S(1)} %cholesky.901), custom_call_target="Cholesky" | custom-call | tf_op jit(solution)/shard_map/jit(cholesky)/cholesky | solution.py:61
  499.4 10.0 %custom-call.100 = f32[1,128,128]{1,2,0:T(8,128)S(1)} custom-call(f32[1,128,128]{2,1,0:T(8,128)S(1)} %get-tuple-element.105), custom_call_target="InvertDiagBlocksLowerTriangular" | custom-call | tf_op jit(solution)/shard_map/jit(cholesky)/cholesky | solution.py:61
  510.9 3.3 convolution_subtract_fusion
  514.3 11.7 %cholesky.715 = f32[128,128]{1,0:T(8,128)S(1)} custom-call(f32[128,128]{1,0:T(8,128)S(1)} %cholesky.906), custom_call_target="Cholesky" | custom-call | tf_op jit(solution)/shard_map/jit(cholesky)/cholesky | solution.py:61
  526.6 9.8 %custom-call.101 = f32[1,128,128]{1,2,0:T(8,128)S(1)} custom-call(f32[1,128,128]{2,1,0:T(8,128)S(1)} %get-tuple-element.102), custom_call_target="InvertDiagBlocksLowerTriangular" | custom-call | tf_op jit(solution)/shard_map/jit(cholesky)/cholesky | solution.py:61
  537.8 3.6 fusion.18
  541.4 12.1 %cholesky.734 = f32[128,128]{1,0:T(8,128)S(1)} custom-call(f32[128,128]{1,0:T(8,128)S(1)} %cholesky.911), custom_call_target="Cholesky" | custom-call | tf_op jit(solution)/shard_map/jit(cholesky)/cholesky | solution.py:61
  554.2 9.8 %custom-call.102 = f32[1,128,128]{1,2,0:T(8,128)S(1)} custom-call(f32[1,128,128]{2,1,0:T(8,128)S(1)} %get-tuple-element.99), custom_call_target="InvertDiagBlocksLowerTriangular" | custom-call | tf_op jit(solution)/shard_map/jit(cholesky)/cholesky | solution.py:61
  565.3 3.8 fusion.21
  569.1 11.7 %cholesky.754 = f32[128,128]{1,0:T(8,128)S(1)} custom-call(f32[128,128]{1,0:T(8,128)S(1)} %cholesky.916), custom_call_target="Cholesky" | custom-call | tf_op jit(solution)/shard_map/jit(cholesky)/cholesky | solution.py:61
  581.5 10.0 %custom-call.103 = f32[1,128,128]{1,2,0:T(8,128)S(1)} custom-call(f32[1,128,128]{2,1,0:T(8,128)S(1)} %get-tuple-element.96), custom_call_target="InvertDiagBlocksLowerTriangular" | custom-call | tf_op jit(solution)/shard_map/jit(cholesky)/cholesky | solution.py:61
  592.8 3.8 fusion.24
  596.6 11.7 %cholesky.774 = f32[128,128]{1,0:T(8,128)S(1)} custom-call(f32[128,128]{1,0:T(8,128)S(1)} %cholesky.921), custom_call_target="Cholesky" | custom-call | tf_op jit(solution)/shard_map/jit(cholesky)/cholesky | solution.py:61
  609.0 9.8 %custom-call.104 = f32[1,128,128]{1,2,0:T(8,128)S(1)} custom-call(f32[1,128,128]{2,1,0:T(8,128)S(1)} %get-tuple-element.93), custom_call_target="InvertDiagBlocksLowerTriangular" | custom-call | tf_op jit(solution)/shard_map/jit(cholesky)/cholesky | solution.py:61
  620.0 4.1 fusion.27
  624.1 11.7 %cholesky.794 = f32[128,128]{1,0:T(8,128)S(1)} custom-call(f32[128,128]{1,0:T(8,128)S(1)} %cholesky.926), custom_call_target="Cholesky" | custom-call | tf_op jit(solution)/shard_map/jit(cholesky)/cholesky | solution.py:61
  636.5 9.8 %custom-call.105 = f32[1,128,128]{1,2,0:T(8,128)S(1)} custom-call(f32[1,128,128]{2,1,0:T(8,128)S(1)} %get-tuple-element.90), custom_call_target="InvertDiagBlocksLowerTriangular" | custom-call | tf_op jit(solution)/shard_map/jit(cholesky)/cholesky | solution.py:61
  647.4 3.6 fusion.30
  650.9 12.2 %cholesky.814 = f32[128,128]{1,0:T(8,128)S(1)} custom-call(f32[128,128]{1,0:T(8,128)S(1)} %cholesky.931), custom_call_target="Cholesky" | custom-call | tf_op jit(solution)/shard_map/jit(cholesky)/cholesky | solution.py:61
  663.7 9.8 %custom-call.106 = f32[1,128,128]{1,2,0:T(8,128)S(1)} custom-call(f32[1,128,128]{2,1,0:T(8,128)S(1)} %get-tuple-element.87), custom_call_target="InvertDiagBlocksLowerTriangular" | custom-call | tf_op jit(solution)/shard_map/jit(cholesky)/cholesky | solution.py:61
  674.6 3.3 fusion.33
  677.9 11.7 %cholesky.834 = f32[128,128]{1,0:T(8,128)S(1)} custom-call(f32[128,128]{1,0:T(8,128)S(1)} %cholesky.936), custom_call_target="Cholesky" | custom-call | tf_op jit(solution)/shard_map/jit(cholesky)/cholesky | solution.py:61
  690.2 9.8 %custom-call.107 = f32[1,128,128]{1,2,0:T(8,128)S(1)} custom-call(f32[1,128,128]{2,1,0:T(8,128)S(1)} %get-tuple-element.84), custom_call_target="InvertDiagBlocksLowerTriangular" | custom-call | tf_op jit(solution)/shard_map/jit(cholesky)/cholesky | solution.py:61
  701.0 2.7 fusion.36
  703.7 11.9 %cholesky.854 = f32[128,128]{1,0:T(8,128)S(1)} custom-call(f32[128,128]{1,0:T(8,128)S(1)} %cholesky.941), custom_call_target="Cholesky" | custom-call | tf_op jit(solution)/shard_map/jit(cholesky)/cholesky | solution.py:61
  716.2 9.8 %custom-call.108 = f32[1,128,128]{1,2,0:T(8,128)S(1)} custom-call(f32[1,128,128]{2,1,0:T(8,128)S(1)} %get-tuple-element.81), custom_call_target="InvertDiagBlocksLowerTriangular" | custom-call | tf_op jit(solution)/shard_map/jit(cholesky)/cholesky | solution.py:61
  726.9 2.3 convolution_subtract_fusion.25
  729.2 11.7 %cholesky.872 = f32[128,128]{1,0:T(8,128)S(1)} custom-call(f32[128,128]{1,0:T(8,128)S(1)} %convolution_subtract_fusion.25), custom_call_target="Cholesky" | custom-call | tf_op jit(solution)/shard_map/jit(cholesky)/cholesky | solution.py:61
  756.7 8.5 select_select_fusion
  765.2 35.2 %while.1 = (s32[]{:T(128)}, f32[1536,1536]{1,0:T(8,128)}, s32[12,2]{0,1:T(2,128)S(1)}, f32[12,128,128]{2,1,0:T(8,128)S(1)}, s32[]{:T(128)}) while((s32[]{:T(128)}, f32[1536,1536]{1,0:T(8,128)}, s32[12,2]{0,1:T(2,128)S(1)}, f32[12,128,128]{2,1,0:T(8,128)S(1)}, s32[]{:T(128)}) %tuple.106), condition=%wide.while_cond, body=%wide.while_body.sunk | while | flops 2 | bytes 131189 | solution.py:63
  765.9 2.2 bitcast_dynamic-update-slice_fusion.2
  768.8 2.2 bitcast_dynamic-update-slice_fusion.2
  800.4 118.3 %custom-call.109 = f32[12,128,128]{1,2,0:T(8,128)S(1)} custom-call(f32[12,128,128]{2,1,0:T(8,128)S(1)} %get-tuple-element.12), custom_call_target="InvertDiagBlocksLowerTriangular" | custom-call | tf_op jit(solution)/shard_map/jit(_solve_triangular)/triangular_solve | solution.py:63
  941.0 2.4 convolution_subtract_fusion.24
  (206 shorter events, 103.2 us)
Async XLA Ops:
  6.5 90.4 %reduce-scatter.2.cloned.1.call-start = ((), (), s32[]{:S(2)}) async-start(), calls=%async_computation.2 | async-start | bytes 6127616 | tf_op jit(solution)/shard_map/reduce_scatter | solution.py:41
  17.2 240.3 %all-reduce.3.cloned.1.call-start = ((), (), s32[]{:S(2)}) async-start(), calls=%async_computation.3 | async-start | bytes 4325376 | tf_op jit(solution)/shard_map/psum | solution.py:57
  127.0 132.5 %copy-start.1 = (f32[96]{0:T(128)S(1)}, f32[96]{0:T(128)}, u32[]{:S(2)}) copy-start(f32[96]{0:T(128)} %param.7) | copy-start | bytes 1156
  127.1 278.9 %all-gather.2.cloned.1.call-start = ((), (), s32[]{:S(2)}) async-start(), calls=%async_computation.4 | async-start | bytes 10027008 | tf_op jit(solution)/shard_map/all_gather | solution.py:59
  920.3 9.7 %copy-start = (f32[1536,1536]{1,0:T(8,128)S(1)}, f32[1536,1536]{1,0:T(8,128)}, u32[]{:S(2)}) copy-start(f32[1536,1536]{1,0:T(8,128)} %get-tuple-element.190) | copy-start | bytes 28311556
Sparse Core Ops, SparseCore 0:
  17.4 79.5 reduce-scatter.1
  127.2 130.2 all-reduce.2
  260.1 145.8 all-gather.1
where the time goes:
time: 970 us; the launch traced here: 965 us
  other arithmetic  409 us (42%)
  waiting for transfers between devices  355 us (37%)
  matrix products  100 us (10%)
  local copies, waits for them, and re-layouts  51.6 us (5%)
  blocking collectives  27.1 us (3%)
  between operations  22.1 us (2%)
    another operation x46, other arithmetic, on_device(): factor = jnp.linalg.cholesky(kernel)  265 us
    all_gather x1, waiting for transfers between devices, on_device(): kernel = lax.all_gather(kernel_block, 'dp', axis=0, tiled=True)  145 us
    psum x1, waiting for transfers between devices, on_device(): summed = lax.psum(partial_value, 'param')  130 us
    another operation x3, other arithmetic, on_device(): jax.scipy.linalg.solve_triangular(factor, forward, lower=True, trans=1)  127 us
    reduce_scatter x1, waiting for transfers between devices, on_device(): lax.psum_scatter(lax.dot_general(projection, stacked, contract_rows, pref...  79.7 us
    another operation x22, matrix products, on_device(): factor = jnp.linalg.cholesky(kernel)  50.1 us
    another operation x36, local copies, waits for them, and re-layouts  35 us
    all_to_all x1, blocking collectives, sent_to_all(): lax.all_to_all(jnp.broadcast_to(x[None], (length, *x.shape)), axis, 0, 0,...  27.1 us
  transfers between devices with their start and end apart: 3, of which 3 were waited for; matrix products, arithmetic and copies ran while one was open for 0% of the time, Pallas kernels for 0%

commit v1 on v0

v1 whole, which is shorter than its diff:
```python
import functools
import math

import jax
import jax.numpy as jnp
from jax import lax
from jax.experimental import pallas as pl
from jax.experimental.pallas import tpu as pltpu
from jax.sharding import PartitionSpec as P

ridge_value = 0.5
BLK = 128
SUB = 16


def split(x):
    hi = x.astype(jnp.bfloat16)
    return hi, (x - hi.astype(jnp.float32)).astype(jnp.bfloat16)


def dot(a, b, ca, cb):
    return lax.dot_general(a, b, (((ca,), (cb,)), ((), ())), preferred_element_type=jnp.float32)


def dot3(ah, al, bh, bl, ca, cb):
    return dot(ah, bh, ca, cb) + (dot(ah, bl, ca, cb) + dot(al, bh, ca, cb))


def factor_block(d_ref):
    rows = lax.broadcasted_iota(jnp.int32, (SUB, BLK), 0)
    for s in range(BLK // SUB):
        top = s * SUB
        left = d_ref[top : top + SUB, :BLK]
        right = d_ref[top : top + SUB, BLK:]
        cols = [jnp.broadcast_to(left[:, top + j : top + j + 1], (SUB, BLK)) for j in range(SUB)]
        for j in range(SUB):
            scale = lax.rsqrt(cols[j][j : j + 1, :])
            lower = jnp.where(rows > j, cols[j] * scale, 0.0)
            row_l = left[j : j + 1, :] * scale
            row_r = right[j : j + 1, :] * scale
            left = jnp.where(rows == j, row_l, left - lower * row_l)
            right = jnp.where(rows == j, row_r, right - lower * row_r)
            for k in range(j + 1, SUB):
                cols[k] = cols[k] - lower * lower[k : k + 1, :]
        both = jnp.concatenate([left, right], axis=1)
        d_ref[top : top + SUB, :] = both
        if s + 1 < BLK // SUB:
            hi, lo = split(both)
            lhs = jnp.concatenate([hi[:, :BLK], lo[:, :BLK], hi[:, :BLK]], axis=0)
            rhs = jnp.concatenate([hi, hi, lo], axis=0)
            update = dot(lhs, rhs, 0, 0)
            d_ref[top + SUB :, :] = d_ref[top + SUB :, :] - update[top + SUB :, :]


def chol_kernel(n, t, inverse, k_ref, y_ref, x_ref, uh, ul, row, diag, ih, il, xh, xl):
    blocks = n // BLK
    width = n + t
    ident = (
        lax.broadcasted_iota(jnp.int32, (BLK, BLK), 0) == lax.broadcasted_iota(jnp.int32, (BLK, BLK), 1)
    ).astype(jnp.float32)

    def step(k, carry):
        for kk in range(blocks):
            first = kk * BLK

            @pl.when(k == kk)
            def _(kk=kk, first=first):
                if kk == 0:
                    row[:, :n] = k_ref[:BLK, :] * inverse
                    row[:, n:] = y_ref[:BLK, :] * inverse
                else:
                    upd = dot3(
                        uh[:first, first : first + BLK],
                        ul[:first, first : first + BLK],
                        uh[:first, first:],
                        ul[:first, first:],
                        0,
                        0,
                    )
                    row[:, first:n] = k_ref[first : first + BLK, first:] * inverse - upd[:, : n - first]
                    row[:, n:] = y_ref[first : first + BLK, :] * inverse - upd[:, n - first :]
                diag[:, :BLK] = row[:, first : first + BLK] + ridge_value * ident

        diag[:, BLK:] = ident
        factor_block(diag)
        inv_h, inv_l = split(diag[:, BLK:])
        at = pl.ds(pl.multiple_of(k * BLK, BLK), BLK)
        ih[at, :] = inv_h
        il[at, :] = inv_l
        for kk in range(blocks):
            last = (kk + 1) * BLK

            @pl.when(k == kk)
            def _(kk=kk, last=last):
                a_h, a_l = split(row[:, last:])
                u = dot3(inv_h, inv_l, a_h, a_l, 1, 0)
                u_h, u_l = split(u)
                uh[last - BLK : last, last:] = u_h
                ul[last - BLK : last, last:] = u_l
                d_h, d_l = split(diag[:, :BLK])
                uh[last - BLK : last, last - BLK : last] = d_h
                ul[last - BLK : last, last - BLK : last] = d_l

        return carry

    lax.fori_loop(0, blocks, step, 0)
    for kk in reversed(range(blocks)):
        first, last = kk * BLK, (kk + 1) * BLK
        rhs = uh[first:last, n:].astype(jnp.float32) + ul[first:last, n:].astype(jnp.float32)
        if kk < blocks - 1:
            rhs = rhs - dot3(uh[first:last, last:n], ul[first:last, last:n], xh[last:, :], xl[last:, :], 1, 0)
        r_h, r_l = split(rhs)
        sol = dot3(ih[first:last, :], il[first:last, :], r_h, r_l, 0, 0)
        s_h, s_l = split(sol)
        xh[first:last, :] = s_h
        xl[first:last, :] = s_l
        x_ref[first:last, :] = sol


def chol_solve(kernel, cross_t, inverse):
    n, t = cross_t.shape
    return pl.pallas_call(
        functools.partial(chol_kernel, n, t, inverse),
        out_shape=jax.ShapeDtypeStruct((n, t), jnp.float32),
        in_specs=[pl.BlockSpec(memory_space=pltpu.VMEM)] * 2,
        out_specs=pl.BlockSpec(memory_space=pltpu.VMEM),
        scratch_shapes=[
            pltpu.VMEM((n, n + t), jnp.bfloat16),
            pltpu.VMEM((n, n + t), jnp.bfloat16),
            pltpu.VMEM((BLK, n + t), jnp.float32),
            pltpu.VMEM((BLK, 2 * BLK), jnp.float32),
            pltpu.VMEM((n, BLK), jnp.bfloat16),
            pltpu.VMEM((n, BLK), jnp.bfloat16),
            pltpu.VMEM((n, t), jnp.bfloat16),
            pltpu.VMEM((n, t), jnp.bfloat16),
        ],
        compiler_params=pltpu.CompilerParams(vmem_limit_bytes=60 * 2**20),
    )(kernel, cross_t)


def on_device(ex_grads, tgt_grads, projection, example_weight):
    ex_rows = ex_grads.shape[0]
    columns = projection.shape[1]
    params = lax.axis_size("param")
    param_pos = lax.axis_index("param")
    replicas = lax.axis_size("dp")
    stacked = jnp.concatenate([ex_grads, tgt_grads], axis=0)
    rows = stacked.shape[0]
    part = lax.dot_general(
        projection, stacked, (((0,), (1,)), ((), ())), preferred_element_type=jnp.float32
    ).astype(jnp.float16)
    parts = lax.all_to_all(part.reshape(params, columns // params, rows), "param", 0, 0, tiled=True)
    features = jnp.sum(parts.astype(jnp.float32), axis=0).astype(jnp.bfloat16)
    mine = features[:, :ex_rows]
    sent = jnp.broadcast_to(mine[None], (replicas, *mine.shape))
    everyone = jnp.moveaxis(lax.all_to_all(sent, "dp", 0, 0, tiled=True), 0, 1)
    everyone = everyone.reshape(mine.shape[0], replicas * ex_rows)
    contract = (((0,), (0,)), ((), ()))
    inner = lax.dot_general(mine, everyone, contract, preferred_element_type=jnp.float32)
    cross_t = lax.dot_general(
        everyone, features[:, ex_rows:], contract, preferred_element_type=jnp.float32
    )
    inner, cross_t = lax.psum((inner, cross_t), "param")
    kernel = lax.all_gather(inner, "dp", axis=0, tiled=True)
    solved = chol_solve(kernel, cross_t, 1.0 / columns)
    block = solved.shape[0] // params
    chosen = lax.dynamic_slice_in_dim(solved, param_pos * block, block, 0)
    return chosen.T * math.sqrt(columns) * example_weight[None, :]


def solution(mesh):
    placed = (P("dp", "param"), P("dp", "param"), P("param", None), P("param"))
    return jax.shard_map(
        on_device, mesh=mesh, in_specs=placed, out_specs=P("dp", "param"), check_vma=False
    )
```

time: 970 us -> 444 us (0.46)
  other arithmetic: 409 us -> 1.99 us
  matrix products: 100 us -> 11 us
  waiting for transfers between devices: 355 us -> 276 us
  Pallas kernels: 0 us -> 67.1 us
  local copies, waits for them, and re-layouts: 51.6 us -> 0.87 us
  blocking collectives: 27.1 us -> 73.4 us
    another operation x49 -> x0, other arithmetic: 391 us -> none  [the longest x46 265 us: on_device(): factor = jnp.linalg.cholesky(kernel)]
    another operation x68 -> x0, matrix products: 87.5 us -> none  [the longest x22 50.1 us: on_device(): factor = jnp.linalg.cholesky(kernel)]
    reduce_scatter x1 -> x0, waiting for transfers between devices: 79.7 us -> none  [on_device(): lax.psum_scatter(lax.dot_general(projection, stacked, contract_rows, pref...]
    pallas_call x0 -> x1, Pallas kernels: none -> 67.1 us  [chol_solve(): pl.pallas_call(functools.partial(chol_kernel, n, t, inverse), out_shape=j...]
    all_to_all x1 -> x2, blocking collectives: 27.1 us -> 73.4 us  [the longest x1 42 us: on_device(): lax.all_to_all(part.reshape(params, columns // params, rows), 'param', 0,...]
    another operation x57 -> x0, local copies, waits for them, and re-layouts: 40.8 us -> none
    div x1 -> x0, other arithmetic: 12.3 us -> none  [on_device(): factor = jnp.linalg.cholesky(kernel)]
    all_gather x1 -> x0, local copies, waits for them, and re-layouts: 10.1 us -> none  [on_device(): kernel = lax.all_gather(kernel_block, 'dp', axis=0, tiled=True)]
  transfers between devices with their start and end apart: 3 -> 2, of which waited for: 3 -> 2; matrix products, arithmetic and copies ran while one was open for 0% -> 0% of each run, Pallas kernels for 0% -> 0%
where the time goes in v1:
time: 444 us
  waiting for transfers between devices  276 us (62%)
  blocking collectives  73.4 us (17%)
  Pallas kernels  67.1 us (15%)
  between operations  13.5 us (3%)
  matrix products  11 us (2%)
    all_gather x1, waiting for transfers between devices, on_device(): kernel = lax.all_gather(inner, 'dp', axis=0, tiled=True)  149 us
    psum x1, waiting for transfers between devices, on_device(): inner, cross_t = lax.psum((inner, cross_t), 'param')  127 us
    pallas_call x1, Pallas kernels, chol_solve(): pl.pallas_call(functools.partial(chol_kernel, n, t, inverse), out_shape=j...  67.1 us
    all_to_all x1, blocking collectives, on_device(): lax.all_to_all(part.reshape(params, columns // params, rows), 'param', 0,...  42 us
    all_to_all x1, blocking collectives, on_device(): everyone = jnp.moveaxis(lax.all_to_all(sent, 'dp', 0, 0, tiled=True), 0, 1)  31.4 us
  transfers between devices with their start and end apart: 2, of which 2 were waited for; matrix products, arithmetic and copies ran while one was open for 0% of the time, Pallas kernels for 0%

profile of v1, /device:TPU:1, one launch (start us, length us, event | category | flops | bytes accessed | tf_op | source)
XLA Modules:
  0.0 443.6 jit_solution(6931506215245669260)
XLA Ops:
  6.5 0.0 all-reduce.3.cloned.1.call-start
  6.5 8.2 %convolution_convert_fusion = f16[352,4096]{1,0:T(8,128)(2,1)S(1)} fusion(bf16[1280,4096]{1,0:T(8,128)(2,1)} %param.6, bf16[256,1280]{1,0:T(8,128)(2,1)} %param.5, bf16[96,1280]{1,0:T(8,128)(2,1)} %param.4), kind=kOutput, calls=%fused_computation.1 | convolution fusion | flops 3694231552 | bytes 14270464 | tf_op jit(solution)/shard_map/dot_general | solution.py:149
  14.8 0.8 copy.8
  15.6 42.0 %all_to_all.10 = f16[16,256,352]{1,2,0:T(8,128)(2,1)S(1)} all-to-all(f16[16,256,352]{1,2,0:T(8,128)(2,1)S(1)} %bitcast.13), channel_id=1, replica_groups=mesh['dp'=16,'param'=16] {'param'}, dimensions={0} | all-to-all | bytes 5767168 | tf_op jit(solution)/shard_map/all_to_all | solution.py:152
  57.5 0.4 convert_reduce_fusion
  57.9 0.1 broadcast_in_dim.2
  58.0 31.4 %all_to_all.11 = bf16[16,256,96]{1,2,0:T(8,128)(2,1)S(1)} all-to-all(bf16[16,256,96]{1,2,0:T(8,128)(2,1)S(1)} %broadcast_in_dim.2), channel_id=1, replica_groups=mesh['dp'=16,'param'=16] {'dp'}, dimensions={0} | all-to-all | bytes 1572864 | tf_op jit(solution)/shard_map/all_to_all | solution.py:156
  89.4 0.0 copy-start
  89.4 1.6 fusion.3
  91.0 1.2 fusion.6
  92.2 0.0 all-reduce.3.cloned.1.call-update
  92.2 0.2 all-gather.2.cloned.1.call-start
  92.4 127.0 %all-reduce.3.cloned.1.call-done = (f32[96,1536]{1,0:T(8,128)}, f32[1536,256]{1,0:T(8,128)}) async-done(((f32[96,1536]{1,0:T(8,128)}, f32[1536,256]{1,0:T(8,128)}), (f32[96,1536]{1,0:T(8,128)}, f32[1536,256]{1,0:T(8,128)})) %all-reduce.3.cloned.1.call-update) | async-done | bytes 2162704 | tf_op jit(solution)/shard_map/psum | solution.py:163
  219.4 0.0 all-gather.2.cloned.1.call-update
  219.5 0.0 copy-done
  219.5 148.6 %all-gather.2.cloned.1.call-done.k_ref = f32[1536,1536]{1,0:T(8,128)} async-done(((f32[96,1536]{1,0:T(8,128)}), f32[1536,1536]{1,0:T(8,128)}) %all-gather.2.cloned.1.call-update) | async-done | bytes 9437200 | tf_op jit(solution)/shard_map/all_gather | solution.py:164
  368.0 67.1 %shard_map.46 = f32[1536,256]{1,0:T(8,128)} custom-call(f32[1536,1536]{1,0:T(8,128)} %all-gather.2.cloned.1.call-done.k_ref, f32[1536,256]{1,0:T(8,128)} %get-tuple-element.6.y_ref), custom_call_target="tpu_custom_call" | custom-call | tf_op jit(solution)/shard_map/pallas_call | solution.py:122
  435.1 1.6 multiply_bitcast_fusion
  (2 shorter events, 0.0 us)
Async XLA Ops:
  6.5 212.9 %all-reduce.3.cloned.1.call-start = ((), (), s32[]{:S(2)}) async-start(), calls=%async_computation.3 | async-start | bytes 4325376 | tf_op jit(solution)/shard_map/psum | solution.py:163
  89.4 130.0 %copy-start = (f32[96]{0:T(128)S(1)}, f32[96]{0:T(128)}, u32[]{:S(2)}) copy-start(f32[96]{0:T(128)} %param.7) | copy-start | bytes 1156
  92.2 275.8 %all-gather.2.cloned.1.call-start = ((), (), s32[]{:S(2)}) async-start(), calls=%async_computation.2 | async-start | bytes 10027008 | tf_op jit(solution)/shard_map/all_gather | solution.py:164
Sparse Core Ops, SparseCore 0:
  92.3 127.0 all-reduce.2
  222.0 145.9 all-gather.1

commit v2 on v1

--- a/solution.py
+++ b/solution.py
@@ -10,6 +10,18 @@
 
 ridge_value = 0.5
 BLK = 128
+MESH_ID = pl.DeviceIdType.MESH
+TILES = 5
+
+
+def tile_place(t):
+    pair, offset = t // 13, t % 13
+    low = (offset + pair) // 12
+    row = pair + low * (11 - 2 * pair)
+    return row, row + offset - low * (12 - pair)
+
+
+TILE_AT = {tile_place(t): t for t in range(78)}
 SUB = 16
 
 
@@ -52,7 +64,7 @@
             d_ref[top + SUB :, :] = d_ref[top + SUB :, :] - update[top + SUB :, :]
 
 
-def chol_kernel(n, t, inverse, k_ref, y_ref, x_ref, uh, ul, row, diag, ih, il, xh, xl):
+def chol_kernel(n, t, inverse, g_ref, c_ref, x_ref, uh, ul, row, diag, ih, il, xh, xl):
     blocks = n // BLK
     width = n + t
     ident = (
@@ -65,9 +77,17 @@
 
             @pl.when(k == kk)
             def _(kk=kk, first=first):
+                rhs = jnp.concatenate(
+                    [c_ref[:, first : first + BLK], jnp.zeros((t - c_ref.shape[0], BLK), jnp.float32)], axis=0
+                )
+                row[:, n:] = rhs.T * inverse
+                for cc in range(kk, blocks):
+                    owner, i = divmod(TILE_AT[kk, cc], TILES)
+                    for p in range(BLK // 8):
+                        piece = g_ref[owner // 8 * 2 + p // 2 % 2, p // 4, owner % 8, p % 2, i]
+                        row[8 * p : 8 * p + 8, cc * BLK : (cc + 1) * BLK] = piece * inverse
                 if kk == 0:
-                    row[:, :n] = k_ref[:BLK, :] * inverse
-                    row[:, n:] = y_ref[:BLK, :] * inverse
+                    pass
                 else:
                     upd = dot3(
                         uh[:first, first : first + BLK],
@@ -77,8 +97,7 @@
                         0,
                         0,
                     )
-                    row[:, first:n] = k_ref[first : first + BLK, first:] * inverse - upd[:, : n - first]
-                    row[:, n:] = y_ref[first : first + BLK, :] * inverse - upd[:, n - first :]
+                    row[:, first:] = row[:, first:] - upd
                 diag[:, :BLK] = row[:, first : first + BLK] + ridge_value * ident
 
         diag[:, BLK:] = ident
@@ -117,8 +136,8 @@
         x_ref[first:last, :] = sol
 
 
-def chol_solve(kernel, cross_t, inverse):
-    n, t = cross_t.shape
+def chol_solve(tiles, cross, inverse):
+    n, t = cross.shape[1], BLK
     return pl.pallas_call(
         functools.partial(chol_kernel, n, t, inverse),
         out_shape=jax.ShapeDtypeStruct((n, t), jnp.float32),
@@ -135,37 +154,223 @@
             pltpu.VMEM((n, t), jnp.bfloat16),
         ],
         compiler_params=pltpu.CompilerParams(vmem_limit_bytes=60 * 2**20),
-    )(kernel, cross_t)
+    )(tiles, cross)
+
+
+def finish(features, ex_rows, example_weight):
+    params = lax.axis_size("param")
+    columns = features.shape[1] * params
+    tiles, cross = spread(features, ex_rows)
+    solved = chol_solve(tiles, cross, 1.0 / columns)[:, : cross.shape[0]]
+    block = solved.shape[0] // params
+    chosen = jnp.swapaxes(solved.reshape(params, block, cross.shape[0]), 1, 2)
+    chosen = lax.all_to_all(chosen, "param", 0, 0, tiled=True)
+    return chosen.reshape(-1, block) * math.sqrt(columns) * example_weight[None, :]
+
+
+def spread_kernel(feat_ref, g_ref, c_ref, fall, kp, kr, ks, kg, cp, cr, cs, cg, send, recv):
+    d, p = lax.axis_index("dp"), lax.axis_index("param")
+    x_hi, z = d // 8, d % 8
+    y, x_lo, core = p // 4, (p // 2) % 2, p % 2
+    x = x_hi * 2 + x_lo
+    way = 1 - 2 * core
+    ex = fall.shape[0] // 16
+
+    def at(x, y, z, core):
+        return ((x // 2) * 8 + z, (y * 2 + x % 2) * 2 + core)
+
+    def turn(v, step, n):
+        return (v + step + n) % n
+
+    count = [0]
+    started = []
+
+    def push(src, dst, device):
+        i = count[0]
+        count[0] += 1
+        copy = pltpu.make_async_remote_copy(
+            src_ref=src,
+            dst_ref=dst,
+            send_sem=send.at[i],
+            recv_sem=recv.at[i],
+            device_id=device,
+            device_id_type=MESH_ID,
+        )
+        copy.start()
+        started.append(copy)
+        return copy
+
+    barrier = pltpu.get_barrier_semaphore()
+    peers = [((d + s) % 16, p) for s in range(1, 16)]
+    peers += [(d, (p + 2 * s) % 16) for s in range(1, 8)]
+    peers += [(d, p + way), at(turn(x, 2 * x_lo - 1, 4), y, z, core)]
+    for peer in peers:
+        pl.semaphore_signal(barrier, inc=1, device_id=peer, device_id_type=MESH_ID)
+
+    def ring(pos, n, block, device):
+        got = []
+        for step in range(1, n // 2 + 1):
+            for copy in got:
+                copy.wait_recv()
+            got = []
+            if step < n // 2:
+                for sign in (1, -1):
+                    ref = block(turn(pos, -sign * (step - 1), n))
+                    got.append(push(ref, ref, device(turn(pos, sign, n))))
+            else:
+                ref = block((pos - way * (step - 1) + n) % n)
+                got.append(push(ref, ref, device((pos + way + n) % n)))
+            yield
+        for copy in got:
+            copy.wait_recv()
+        yield
+
+    def run(*rings):
+        live = list(rings)
+        while live:
+            for one in list(live):
+                if next(one, "end") == "end":
+                    live.remove(one)
+
+    def feat_rows(hi, zz):
+        return fall.at[pl.ds(pl.multiple_of((hi * 8 + zz) * ex, ex), ex), :]
+
+    mine = pl.ds(pl.multiple_of(d * ex, ex), ex)
+    fall[mine, :] = feat_ref[:ex, :]
+    pl.semaphore_wait(barrier, len(peers))
+
+    other = (x_hi + 1) % 2
+
+    def far_ring():
+        ref = feat_rows(x_hi, z)
+        copy = push(ref, ref, at(turn(x, 2, 4), y, z, core))
+        yield
+        copy.wait_recv()
+        yield from ring(z, 8, lambda zz: feat_rows(other, zz), lambda zz: at(x, y, zz, core))
+
+    run(
+        far_ring(),
+        ring(z, 8, lambda zz: feat_rows(x_hi, zz), lambda zz: at(x, y, zz, core)),
+    )
+
+    nt = (((1,), (1,)), ((), ()))
+    for i in range(TILES):
+        row, col = tile_place((d * TILES + i) % 78)
+        a = fall[pl.ds(pl.multiple_of(row * 128, 128), 128), :]
+        b = fall[pl.ds(pl.multiple_of(col * 128, 128), 128), :]
+        tile = lax.dot_general(a, b, nt, preferred_element_type=jnp.float32)
+        kp[:, :, i] = tile.reshape(8, 2, 8, 128)
+    k_core = push(kp.at[:, 1 - core], kr, (d, p + way))
+    cross = lax.dot_general(feat_ref[ex:, :], fall[...], nt, preferred_element_type=jnp.float32)
+    cp[...] = cross.reshape(cp.shape)
+    c_core = push(cp.at[:, 1 - core], cr, (d, p + way))
+
+    chip = p // 2
+
+    def chips(pieces, landing):
+        return [
+            push(pieces.at[(chip + s) % 8], landing.at[s - 1], (d, (p + 2 * s) % 16))
+            for s in (4, 5, 3, 2, 6, 1, 7)
+        ]
+
+    k_core.wait_recv()
+    ks[...] = kp[:, core] + kr[...]
+    k_parts = chips(ks, kg)
+    c_core.wait_recv()
+    cs[...] = cp[:, core] + cr[...]
+    for copy in k_parts:
+        copy.wait_recv()
+    total = ks[chip]
+    for s in range(7):
+        total = total + kg[s]
+    g_ref[x, y, z, core] = total
+    c_parts = chips(cs, cg)
+
+    run(ring(z, 8, lambda zz: g_ref.at[x, y, zz, core], lambda zz: at(x, y, zz, core)))
+    low, high = pl.ds(0, 4), pl.ds(4, 4)
+    run(
+        ring(x, 4, lambda xx: g_ref.at[xx, y, low, core], lambda xx: at(xx, y, z, core)),
+        ring(y, 4, lambda yy: g_ref.at[x, yy, high, core], lambda yy: at(x, yy, z, core)),
+    )
+    pair = (d, p + way)
+    shared = []
+
+    def pass_on(ref):
+        shared.append(push(ref, ref, pair))
+
+    pass_on(g_ref.at[:, y, low, core])
+    pass_on(g_ref.at[x, :, high, core])
+    last_y = lambda yy: g_ref.at[:, yy, low, core]
+    last_x = lambda xx: g_ref.at[xx, :, high, core]
+    ring_y = ring(y, 4, last_y, lambda yy: at(x, yy, z, core))
+    ring_x = ring(x, 4, last_x, lambda xx: at(xx, y, z, core))
+    next(ring_y)
+    next(ring_x)
+    next(ring_y)
+    for sign in (1, -1):
+        pass_on(last_y(turn(y, sign, 4)))
+    next(ring_x)
+    for sign in (1, -1):
+        pass_on(last_x(turn(x, sign, 4)))
+    next(ring_y)
+    pass_on(last_y(turn(y, 2, 4)))
+    next(ring_x)
+    pass_on(last_x(turn(x, 2, 4)))
+    for copy in c_parts:
+        copy.wait_recv()
+    whole = cs[chip]
+    for s in range(7):
+        whole = whole + cg[s]
+    c_ref[...] = whole
+    for copy in shared:
+        copy.wait_recv()
+    for copy in started:
+        copy.wait_send()
+
+
+def spread(features, ex):
+    width = features.shape[1]
+    tgt = (features.shape[0] - ex) // 16
+    n = 16 * ex
+    f32 = jnp.float32
+    return pl.pallas_call(
+        spread_kernel,
+        out_shape=(
+            jax.ShapeDtypeStruct((4, 4, 8, 2, TILES, 8, 128), f32),
+            jax.ShapeDtypeStruct((tgt, n), f32),
+        ),
+        in_specs=[pl.BlockSpec(memory_space=pltpu.VMEM)],
+        out_specs=(pl.BlockSpec(memory_space=pltpu.VMEM), pl.BlockSpec(memory_space=pltpu.VMEM)),
+        scratch_shapes=[
+            pltpu.VMEM((n, width), jnp.bfloat16),
+            pltpu.VMEM((8, 2, TILES, 8, 128), f32),
+            pltpu.VMEM((8, TILES, 8, 128), f32),
+            pltpu.VMEM((8, TILES, 8, 128), f32),
+            pltpu.VMEM((7, TILES, 8, 128), f32),
+            pltpu.VMEM((8, 2, tgt, n), f32),
+            pltpu.VMEM((8, tgt, n), f32),
+            pltpu.VMEM((8, tgt, n), f32),
+            pltpu.VMEM((7, tgt, n), f32),
+            pltpu.SemaphoreType.DMA((60,)),
+            pltpu.SemaphoreType.DMA((60,)),
+        ],
+        compiler_params=pltpu.CompilerParams(
+            collective_id=0, has_side_effects=True, vmem_limit_bytes=60 * 2**20
+        ),
+    )(features)
 
 
 def on_device(ex_grads, tgt_grads, projection, example_weight):
     ex_rows = ex_grads.shape[0]
     columns = projection.shape[1]
     params = lax.axis_size("param")
-    param_pos = lax.axis_index("param")
-    replicas = lax.axis_size("dp")
     stacked = jnp.concatenate([ex_grads, tgt_grads], axis=0)
     rows = stacked.shape[0]
-    part = lax.dot_general(
-        projection, stacked, (((0,), (1,)), ((), ())), preferred_element_type=jnp.float32
-    ).astype(jnp.float16)
-    parts = lax.all_to_all(part.reshape(params, columns // params, rows), "param", 0, 0, tiled=True)
+    part = jnp.dot(stacked, projection, preferred_element_type=jnp.float32).astype(jnp.float16)
+    part = jnp.moveaxis(part.reshape(rows, params, columns // params), 1, 0)
+    parts = lax.all_to_all(part, "param", 0, 0, tiled=True)
     features = jnp.sum(parts.astype(jnp.float32), axis=0).astype(jnp.bfloat16)
-    mine = features[:, :ex_rows]
-    sent = jnp.broadcast_to(mine[None], (replicas, *mine.shape))
-    everyone = jnp.moveaxis(lax.all_to_all(sent, "dp", 0, 0, tiled=True), 0, 1)
-    everyone = everyone.reshape(mine.shape[0], replicas * ex_rows)
-    contract = (((0,), (0,)), ((), ()))
-    inner = lax.dot_general(mine, everyone, contract, preferred_element_type=jnp.float32)
-    cross_t = lax.dot_general(
-        everyone, features[:, ex_rows:], contract, preferred_element_type=jnp.float32
-    )
-    inner, cross_t = lax.psum((inner, cross_t), "param")
-    kernel = lax.all_gather(inner, "dp", axis=0, tiled=True)
-    solved = chol_solve(kernel, cross_t, 1.0 / columns)
-    block = solved.shape[0] // params
-    chosen = lax.dynamic_slice_in_dim(solved, param_pos * block, block, 0)
-    return chosen.T * math.sqrt(columns) * example_weight[None, :]
+    return finish(features, ex_rows, example_weight)
 
 
 def solution(mesh):

time: 444 us -> 207 us (0.47)
  waiting for transfers between devices: 276 us -> 6.11 us
  Pallas kernels: 67.1 us -> 142 us
  blocking collectives: 73.4 us -> 42 us
  between operations: 13.5 us -> 0.06 us
    all_gather x1 -> x0, waiting for transfers between devices: 149 us -> none  [on_device(): kernel = lax.all_gather(inner, 'dp', axis=0, tiled=True)]
    psum x1 -> x0, waiting for transfers between devices: 127 us -> none  [on_device(): inner, cross_t = lax.psum((inner, cross_t), 'param')]
    pallas_call x0 -> x1, Pallas kernels: none -> 80.1 us  [spread(): pl.pallas_call(spread_kernel, out_shape=(jax.ShapeDtypeStruct((4, 4, 8, 2...]
    all_to_all x2 -> x1, blocking collectives: 73.4 us -> 42 us  [on_device(): parts = lax.all_to_all(part, 'param', 0, 0, tiled=True)]
    all_to_all x0 -> x1, waiting for transfers between devices: none -> 6.11 us  [finish(): chosen = lax.all_to_all(chosen, 'param', 0, 0, tiled=True)]
    pallas_call x1, Pallas kernels: 67.1 us -> 62.1 us  [chol_solve(): pl.pallas_call(functools.partial(chol_kernel, n, t, inverse), out_shape=j...]
    dot_general x3 -> x1, matrix products: 11 us -> 8.21 us  [on_device(): jnp.dot(stacked, projection, preferred_element_type=jnp.float32)]
  transfers between devices with their start and end apart: 2 -> 1, of which waited for: 2 -> 1; matrix products, arithmetic and copies ran while one was open for 0% -> 0% of each run, Pallas kernels for 0% -> 0%
where the time goes in v2:
time: 207 us
  Pallas kernels  142 us (69%)
  blocking collectives  42 us (20%)
  matrix products  8.21 us (4%)
  waiting for transfers between devices  6.11 us (3%)
  local copies, waits for them, and re-layouts  3.55 us (2%)
  starting transfers between devices  3.41 us (2%)
    pallas_call x1, Pallas kernels, spread(): pl.pallas_call(spread_kernel, out_shape=(jax.ShapeDtypeStruct((4, 4, 8, 2...  80.1 us
    pallas_call x1, Pallas kernels, chol_solve(): pl.pallas_call(functools.partial(chol_kernel, n, t, inverse), out_shape=j...  62.1 us
    all_to_all x1, blocking collectives, on_device(): parts = lax.all_to_all(part, 'param', 0, 0, tiled=True)  42 us
    dot_general x1, matrix products, on_device(): jnp.dot(stacked, projection, preferred_element_type=jnp.float32)  8.21 us
    all_to_all x1, waiting for transfers between devices, finish(): chosen = lax.all_to_all(chosen, 'param', 0, 0, tiled=True)  6.11 us
  transfers between devices with their start and end apart: 1, of which 1 were waited for; matrix products, arithmetic and copies ran while one was open for 0% of the time, Pallas kernels for 0%

profile of v2, /device:TPU:1, one launch (start us, length us, event | category | flops | bytes accessed | tf_op | source)
XLA Modules:
  0.0 206.5 jit_solution(17248133380355864710)
XLA Ops:
  0.0 8.2 %convolution_convert_fusion = f16[352,4096]{1,0:T(8,128)(2,1)S(1)} fusion(bf16[1280,4096]{1,0:T(8,128)(2,1)} %param.6, bf16[256,1280]{1,0:T(8,128)(2,1)} %param.5, bf16[96,1280]{1,0:T(8,128)(2,1)} %param.4), kind=kOutput, calls=%fused_computation.1 | convolution fusion | flops 3694231552 | bytes 14270464 | tf_op jit(solution)/shard_map/dot_general | solution.py:369
  8.2 0.8 copy.13
  9.0 42.0 %all_to_all.10 = f16[16,352,256]{2,1,0:T(8,128)(2,1)S(1)} all-to-all(f16[16,352,256]{2,1,0:T(8,128)(2,1)S(1)} %bitcast.13), channel_id=1, replica_groups=mesh['dp'=16,'param'=16] {'param'}, dimensions={0} | all-to-all | bytes 5767168 | tf_op jit(solution)/shard_map/all_to_all | solution.py:371
  51.0 1.0 convert_reduce_fusion.feat_ref
  52.0 80.1 %shard_map.46 = (f32[4,4,8,2,5,8,128]{6,5,4,3,2,1,0:T(8,128)}, f32[16,1536]{1,0:T(8,128)}) custom-call(bf16[352,256]{1,0:T(8,128)(2,1)} %convert_reduce_fusion.feat_ref), custom_call_target="tpu_custom_call" | custom-call | tf_op jit(solution)/shard_map/pallas_call | solution.py:336
  132.1 0.0 copy-start
  132.1 62.1 %shard_map.47 = f32[1536,128]{1,0:T(8,128)} custom-call(f32[4,4,8,2,5,8,128]{6,5,4,3,2,1,0:T(8,128)} %get-tuple-element.7.g_ref, f32[16,1536]{1,0:T(8,128)} %get-tuple-element.8.c_ref), custom_call_target="tpu_custom_call" | custom-call | tf_op jit(solution)/shard_map/pallas_call | solution.py:141
  194.2 2.0 copy.9
  196.2 3.4 %all-to-all-start.1 = ((f32[16,16,96]{2,1,0:T(8,128)}), f32[16,16,96]{2,1,0:T(8,128)S(1)}, u32[]{:S(2)}, u32[]{:S(2)}) async-start(f32[16,16,96]{2,1,0:T(8,128)} %bitcast.2), calls=%async_computation.1 | async-start | bytes 262144 | tf_op jit(solution)/shard_map/all_to_all | solution.py:167
  199.7 0.0 copy-done
  199.7 6.1 %all-to-all-done.1 = f32[16,16,96]{2,1,0:T(8,128)S(1)} async-done(((f32[16,16,96]{2,1,0:T(8,128)}), f32[16,16,96]{2,1,0:T(8,128)S(1)}, u32[]{:S(2)}, u32[]{:S(2)}) %all-to-all-start.1) | async-done | bytes 98336 | tf_op jit(solution)/shard_map/all_to_all | solution.py:167
  205.8 0.7 copy.10
  (2 shorter events, 0.0 us)
Async XLA Ops:
  132.1 67.6 %copy-start = (f32[96]{0:T(128)S(1)}, f32[96]{0:T(128)}, u32[]{:S(2)}) copy-start(f32[96]{0:T(128)} %param.7) | copy-start | bytes 1156
  196.2 9.5 %all-to-all-start.1 = ((f32[16,16,96]{2,1,0:T(8,128)}), f32[16,16,96]{2,1,0:T(8,128)S(1)}, u32[]{:S(2)}, u32[]{:S(2)}) async-start(f32[16,16,96]{2,1,0:T(8,128)} %bitcast.2), calls=%async_computation.1 | async-start | bytes 262144 | tf_op jit(solution)/shard_map/all_to_all | solution.py:167

commit v3 on v1

v3 whole, which is shorter than its diff:
```python
import functools
import math

import jax
import jax.numpy as jnp
from jax import lax
from jax.experimental import pallas as pl
from jax.experimental.pallas import tpu as pltpu
from jax.sharding import PartitionSpec as P

ridge_value = 0.5
BLK = 128
SUB = 16
TILES = 5
LATE_SUM = 8
F32, BF16 = jnp.float32, jnp.bfloat16


def tile_place(t):
    pair, offset = t // 13, t % 13
    low = (offset + pair) // 12
    row = pair + low * (11 - 2 * pair)
    return row, row + offset - low * (12 - pair)


TILE_AT = {tile_place(t): t for t in range(78)}


def split(x):
    hi = x.astype(BF16)
    return hi, (x - hi.astype(F32)).astype(BF16)


def dot(a, b, ca, cb):
    return lax.dot_general(a, b, (((ca,), (cb,)), ((), ())), preferred_element_type=F32)


def dot3(ah, al, bh, bl, ca, cb):
    return dot(ah, bh, ca, cb) + (dot(ah, bl, ca, cb) + dot(al, bh, ca, cb))


def factor_block(d_ref):
    rows = lax.broadcasted_iota(jnp.int32, (SUB, BLK), 0)
    for s in range(BLK // SUB):
        top = s * SUB
        left = d_ref[top : top + SUB, :BLK]
        right = d_ref[top : top + SUB, BLK:]
        cols = [jnp.broadcast_to(left[:, top + j : top + j + 1], (SUB, BLK)) for j in range(SUB)]
        for j in range(SUB):
            scale = lax.rsqrt(cols[j][j : j + 1, :])
            lower = jnp.where(rows > j, cols[j] * scale, 0.0)
            row_l = left[j : j + 1, :] * scale
            row_r = right[j : j + 1, :] * scale
            left = jnp.where(rows == j, row_l, left - lower * row_l)
            right = jnp.where(rows == j, row_r, right - lower * row_r)
            for k in range(j + 1, SUB):
                cols[k] = cols[k] - lower * lower[k : k + 1, :]
        both = jnp.concatenate([left, right], axis=1)
        d_ref[top : top + SUB, :] = both
        if s + 1 < BLK // SUB:
            hi, lo = split(both)
            lhs = jnp.concatenate([hi[:, :BLK], lo[:, :BLK], hi[:, :BLK]], axis=0)
            rhs = jnp.concatenate([hi, hi, lo], axis=0)
            update = dot(lhs, rhs, 0, 0)
            d_ref[top + SUB :, :] = d_ref[top + SUB :, :] - update[top + SUB :, :]


def scores_kernel(
    inverse, out_scale, ex_ref, tgt_ref, proj_ref, w_ref, o_ref,
    stack, pv, ep, er, eg, tp, tr, tg, fall, tfeat, kp, kr, kg, g, cp, cr, cg,
    uh, ul, row, diag, ih, il, yh, yl, xh, xl, xo, og, load, send, recv,
):
    d, p = lax.axis_index("dp"), lax.axis_index("param")
    x_hi, z = d // 8, d % 8
    y, x_lo, core = p // 4, (p // 2) % 2, p % 2
    x = x_hi * 2 + x_lo
    way = 1 - 2 * core
    chip = p // 2
    pair = (d, p + way)
    n, width = fall.shape
    ex = n // 16
    blocks = n // BLK

    def at(x, y, z, core):
        return ((x // 2) * 8 + z, (y * 2 + x % 2) * 2 + core)

    def turn(v, step, n):
        return (v + step + n) % n

    started = []

    def push(src, dst, device, now=True):
        i = len(started)
        copy = pltpu.make_async_remote_copy(
            src_ref=src,
            dst_ref=dst,
            send_sem=send.at[i],
            recv_sem=recv.at[i],
            device_id=device,
            device_id_type=pl.DeviceIdType.MESH,
        )
        if now:
            copy.start()
        started.append(copy)
        return copy

    def landed(copies):
        for copy in copies:
            copy.wait_recv()

    def ring(pos, n, block, device):
        got = []
        for step in range(1, n // 2 + 1):
            landed(got)
            got = []
            if step < n // 2:
                for sign in (1, -1):
                    ref = block(turn(pos, -sign * (step - 1), n))
                    got.append(push(ref, ref, device(turn(pos, sign, n))))
            else:
                ref = block((pos - way * (step - 1) + n) % n)
                got.append(push(ref, ref, device((pos + way + n) % n)))
            yield
        landed(got)
        yield

    def run(*rings):
        live = list(rings)
        while live:
            for one in list(live):
                if next(one, "end") == "end":
                    live.remove(one)

    def chips(pieces, landing, steps=(4, 5, 3, 2, 6, 1, 7), now=True):
        return [
            push(pieces.at[(chip + s) % 8], landing.at[s - 1], (d, (p + 2 * s) % 16), now) for s in steps
        ]

    def summed(pieces, landing):
        total = pieces[chip]
        for s in range(7):
            total = total + landing[s]
        return total

    barrier = pltpu.get_barrier_semaphore()
    peers = [((d + s) % 16, p) for s in range(1, 16)]
    peers += [(d, (p + s) % 16) for s in range(1, 16)]
    peers += [at(turn(x, 2 * x_lo - 1, 4), y, z, core)]
    for peer in peers:
        pl.semaphore_signal(barrier, inc=1, device_id=peer, device_id_type=pl.DeviceIdType.MESH)

    loads = [
        pltpu.make_async_copy(ex_ref, stack.at[:ex], load.at[16]),
        pltpu.make_async_copy(tgt_ref, stack.at[ex:], load.at[17]),
    ]
    for j in range(16):
        owner = 2 * (j % 8) + (1 - core if j < 8 else core)
        span = pl.ds(pl.multiple_of(owner * width, width), width)
        loads.append(pltpu.make_async_copy(proj_ref.at[:, span], pv.at[j], load.at[j]))
    for copy in loads:
        copy.start()
    loads[0].wait()
    loads[1].wait()
    pl.semaphore_wait(barrier, len(peers))

    e_pair = []
    for j in range(16):
        loads[2 + j].wait()
        part = dot(stack[...], pv[j], 1, 0)
        side = 0 if j < 8 else 1
        ep[side, j % 8] = part[:ex]
        tp[side, j % 8] = part[ex:]
        if j < 8:
            e_pair.append(push(ep.at[0, j], er.at[j], pair))
    t_pair = push(tp.at[0], tr, pair)
    landed(e_pair)
    er[...] = er[...] + ep[1]
    e_parts = chips(er, eg)
    landed([t_pair])
    tr[...] = tr[...] + tp[1]
    landed(e_parts)
    mine = pl.ds(pl.multiple_of(d * ex, ex), ex)
    fall[mine, :] = summed(er, eg).astype(BF16)
    t_parts = chips(tr, tg, (4, 2, 6))

    def feat_rows(hi, zz):
        return fall.at[pl.ds(pl.multiple_of((hi * 8 + zz) * ex, ex), ex), :]

    other = (x_hi + 1) % 2

    def far_ring():
        ref = feat_rows(x_hi, z)
        copy = push(ref, ref, at(turn(x, 2, 4), y, z, core))
        yield
        copy.wait_recv()
        yield from ring(z, 8, lambda zz: feat_rows(other, zz), lambda zz: at(x, y, zz, core))

    run(
        far_ring(),
        ring(z, 8, lambda zz: feat_rows(x_hi, zz), lambda zz: at(x, y, zz, core)),
    )

    for i in range(TILES):
        r, c = tile_place((d * TILES + i) % 78)
        a = fall[pl.ds(pl.multiple_of(r * BLK, BLK), BLK), :]
        b = fall[pl.ds(pl.multiple_of(c * BLK, BLK), BLK), :]
        kp[:, :, i] = dot(a, b, 1, 1).reshape(8, 2, 8, BLK)
    k_pair = push(kp.at[:, 1 - core], kr, pair)
    landed([k_pair])
    kr[...] = kr[...] + kp[:, core]
    landed(chips(kr, kg))
    g[x, y, z, core] = summed(kr, kg)

    run(ring(z, 8, lambda zz: g.at[x, y, zz, core], lambda zz: at(x, y, zz, core)))
    low, high = pl.ds(0, 4), pl.ds(4, 4)
    run(
        ring(x, 4, lambda xx: g.at[xx, y, low, core], lambda xx: at(xx, y, z, core)),
        ring(y, 4, lambda yy: g.at[x, yy, high, core], lambda yy: at(x, yy, z, core)),
    )
    shared = []

    def pass_on(ref):
        shared.append(push(ref, ref, pair))

    def last_y(yy):
        return g.at[:, yy, low, core]

    def last_x(xx):
        return g.at[xx, :, high, core]

    pass_on(last_y(y))
    pass_on(last_x(x))
    ring_y = ring(y, 4, last_y, lambda yy: at(x, yy, z, core))
    ring_x = ring(x, 4, last_x, lambda xx: at(xx, y, z, core))
    next(ring_y)
    next(ring_x)
    next(ring_y)
    for sign in (1, -1):
        pass_on(last_y(turn(y, sign, 4)))
    next(ring_x)
    for sign in (1, -1):
        pass_on(last_x(turn(x, sign, 4)))
    next(ring_y)
    pass_on(last_y(turn(y, 2, 4)))
    next(ring_x)
    pass_on(last_x(turn(x, 2, 4)))
    landed(shared)
    t_parts += chips(tr, tg, (5, 3, 1, 7))

    ident = (
        lax.broadcasted_iota(jnp.int32, (BLK, BLK), 0) == lax.broadcasted_iota(jnp.int32, (BLK, BLK), 1)
    ).astype(F32)
    c_pair = push(cp.at[:, 1 - core], cr, pair, False)
    c_parts = chips(cr, cg, now=False)

    def step(k, carry):
        @pl.when(k == LATE_SUM)
        def _():
            landed(t_parts)
            tfeat[...] = summed(tr, tg).astype(BF16)
            cp[...] = dot(tfeat[...], fall[...], 1, 1).reshape(cp.shape)
            c_pair.start()

        @pl.when(k == LATE_SUM + 1)
        def _():
            landed([c_pair])
            cr[...] = cr[...] + cp[:, core]
            for copy in c_parts:
                copy.start()

        for kk in range(blocks):
            first = kk * BLK

            @pl.when(k == kk)
            def _(kk=kk, first=first):
                for cc in range(kk, blocks):
                    owner, i = divmod(TILE_AT[kk, cc], TILES)
                    for q in range(BLK // 8):
                        piece = g[owner // 8 * 2 + q // 2 % 2, q // 4, owner % 8, q % 2, i]
                        row[8 * q : 8 * q + 8, cc * BLK : (cc + 1) * BLK] = piece * inverse
                if kk:
                    upd = dot3(
                        uh[:first, first : first + BLK],
                        ul[:first, first : first + BLK],
                        uh[:first, first:],
                        ul[:first, first:],
                        0,
                        0,
                    )
                    row[:, first:] = row[:, first:] - upd
                diag[:, :BLK] = row[:, first : first + BLK] + ridge_value * ident

        diag[:, BLK:] = ident
        factor_block(diag)
        inv_h, inv_l = split(diag[:, BLK:])
        place = pl.ds(pl.multiple_of(k * BLK, BLK), BLK)
        ih[place, :] = inv_h
        il[place, :] = inv_l
        for kk in range(blocks - 1):
            last = (kk + 1) * BLK

            @pl.when(k == kk)
            def _(last=last):
                a_h, a_l = split(row[:, last:])
                u_h, u_l = split(dot3(inv_h, inv_l, a_h, a_l, 1, 0))
                uh[last - BLK : last, last:] = u_h
                ul[last - BLK : last, last:] = u_l

        return carry

    lax.fori_loop(0, blocks, step, 0)

    landed(c_parts)
    cross = summed(cr, cg) * inverse

    def against(vh, vl, mh, ml, cm):
        both = dot(jnp.concatenate([vh, vl], axis=0), mh, 1, cm)
        half = vh.shape[0]
        return both[:half] + (both[half:] + dot(vh, ml, 1, cm))

    for kk in range(blocks):
        first, last = kk * BLK, (kk + 1) * BLK
        v = cross[:, first:last]
        if kk:
            v = v - against(yh[:, :first], yl[:, :first], uh[:first, first:last], ul[:first, first:last], 0)
        v_h, v_l = split(v)
        v = against(v_h, v_l, ih[first:last, :], il[first:last, :], 1)
        v_h, v_l = split(v)
        yh[:, first:last] = v_h
        yl[:, first:last] = v_l
    for kk in reversed(range(blocks)):
        first, last = kk * BLK, (kk + 1) * BLK
        v = yh[:, first:last].astype(F32) + yl[:, first:last].astype(F32)
        if kk < blocks - 1:
            v = v - against(xh[:, last:], xl[:, last:], uh[first:last, last:], ul[first:last, last:], 1)
        v_h, v_l = split(v)
        v = against(v_h, v_l, ih[first:last, :], il[first:last, :], 0)
        v_h, v_l = split(v)
        xh[:, first:last] = v_h
        xl[:, first:last] = v_l
        row[:16, first:last] = v

    for q in range(16):
        xo[q, :, :ex] = row[:16, q * ex : (q + 1) * ex]
    finals = [push(xo.at[(p + s) % 16], og.at[s - 1], (d, (p + s) % 16)) for s in range(1, 16)]
    weight = w_ref[...] * out_scale
    o_ref[pl.ds(pl.multiple_of(p * 16, 16), 16), :] = xo[p][:, :ex] * weight
    for s in range(1, 16):
        finals[s - 1].wait_recv()
        o_ref[pl.ds(pl.multiple_of((p + 16 - s) % 16 * 16, 16), 16), :] = og[s - 1][:, :ex] * weight
    for copy in started:
        copy.wait_send()


def on_device(ex_grads, tgt_grads, projection, example_weight):
    ex, depth = ex_grads.shape
    tgt = tgt_grads.shape[0]
    columns = projection.shape[1]
    n, width, rhs = 16 * ex, columns // 16, tgt // 16
    vmem, anywhere = pl.BlockSpec(memory_space=pltpu.VMEM), pl.BlockSpec(memory_space=pl.ANY)
    scratch = [
        ((ex + tgt, depth), BF16),
        ((16, depth, width), BF16),
        ((2, 8, ex, width), F32),
        ((8, ex, width), F32),
        ((7, ex, width), F32),
        ((2, 8, tgt, width), F32),
        ((8, tgt, width), F32),
        ((7, tgt, width), F32),
        ((n, width), BF16),
        ((tgt, width), BF16),
        ((8, 2, TILES, 8, BLK), F32),
        ((8, TILES, 8, BLK), F32),
        ((7, TILES, 8, BLK), F32),
        ((4, 4, 8, 2, TILES, 8, BLK), F32),
        ((8, 2, rhs, n), F32),
        ((8, rhs, n), F32),
        ((7, rhs, n), F32),
        ((n, n), BF16),
        ((n, n), BF16),
        ((BLK, n), F32),
        ((BLK, 2 * BLK), F32),
        ((n, BLK), BF16),
        ((n, BLK), BF16),
        ((rhs, n), BF16),
        ((rhs, n), BF16),
        ((rhs, n), BF16),
        ((rhs, n), BF16),
        ((16, rhs, BLK), F32),
        ((15, rhs, BLK), F32),
    ]
    return pl.pallas_call(
        functools.partial(scores_kernel, 1.0 / columns, math.sqrt(columns)),
        out_shape=jax.ShapeDtypeStruct((tgt, ex), F32),
        in_specs=[anywhere, anywhere, anywhere, vmem],
        out_specs=vmem,
        scratch_shapes=[pltpu.VMEM(*one) for one in scratch]
        + [
            pltpu.SemaphoreType.DMA((18,)),
            pltpu.SemaphoreType.DMA((96,)),
            pltpu.SemaphoreType.DMA((96,)),
        ],
        compiler_params=pltpu.CompilerParams(
            collective_id=0, has_side_effects=True, vmem_limit_bytes=63 * 2**20
        ),
    )(ex_grads, tgt_grads, projection, example_weight.reshape(1, ex))


def solution(mesh):
    placed = (P("dp", "param"), P("dp", "param"), P("param", None), P("param"))
    return jax.shard_map(
        on_device, mesh=mesh, in_specs=placed, out_specs=P("dp", "param"), check_vma=False
    )
```

time: 444 us -> 165 us (0.37)
  waiting for transfers between devices: 276 us -> 0 us
  Pallas kernels: 67.1 us -> 163 us
  blocking collectives: 73.4 us -> 0 us
  between operations: 13.5 us -> 0.01 us
  matrix products: 11 us -> 0 us
    all_gather x1 -> x0, waiting for transfers between devices: 149 us -> none  [on_device(): kernel = lax.all_gather(inner, 'dp', axis=0, tiled=True)]
    psum x1 -> x0, waiting for transfers between devices: 127 us -> none  [on_device(): inner, cross_t = lax.psum((inner, cross_t), 'param')]
    pallas_call x1, Pallas kernels: 67.1 us -> 163 us  [on_device(): pl.pallas_call(functools.partial(scores_kernel, 1.0 / columns, math.sqrt(...]
    all_to_all x2 -> x0, blocking collectives: 73.4 us -> none  [the longest x1 42 us: on_device(): lax.all_to_all(part.reshape(params, columns // params, rows), 'param', 0,...]
    dot_general x3 -> x0, matrix products: 11 us -> none  [the longest x1 8.21 us: on_device(): lax.dot_general(projection, stacked, (((0,), (1,)), ((), ())), preferred_...]
  transfers between devices with their start and end apart: 2 -> 0, of which waited for: 2 -> 0; matrix products, arithmetic and copies ran while one was open for 0% -> 0% of each run, Pallas kernels for 0% -> 0%
where the time goes in v3:
time: 165 us
  Pallas kernels  163 us (99%)
    pallas_call x1, Pallas kernels, on_device(): pl.pallas_call(functools.partial(scores_kernel, 1.0 / columns, math.sqrt(...  163 us

profile of v3, /device:TPU:1, one launch (start us, length us, event | category | flops | bytes accessed | tf_op | source)
XLA Modules:
  0.0 164.9 jit_solution(12711928168205545393)
XLA Ops:
  0.0 163.2 %shard_map.46 = f32[256,96]{1,0:T(8,128)} custom-call(bf16[96,1280]{1,0:T(8,128)(2,1)} %ex_ref.1, bf16[256,1280]{1,0:T(8,128)(2,1)} %tgt_ref.1, bf16[1280,4096]{1,0:T(8,128)(2,1)} %proj_ref.1, f32[1,96]{1,0:T(1,128)} %bitcast.1), custom_call_target="tpu_custom_call" | custom-call | tf_op jit(solution)/shard_map/pallas_call | solution.py:392
  163.2 1.6 copy.5

commit v4 on v3

--- a/solution.py
+++ b/solution.py
@@ -143,41 +143,38 @@
         return total
 
     barrier = pltpu.get_barrier_semaphore()
-    peers = [((d + s) % 16, p) for s in range(1, 16)]
+    peers = [at(x, y, (z + s) % 8, core) for s in range(1, 8)]
     peers += [(d, (p + s) % 16) for s in range(1, 16)]
-    peers += [at(turn(x, 2 * x_lo - 1, 4), y, z, core)]
+    peers += [at(turn(x, 2 * x_lo - 1, 4), y, z, core), at(turn(x, 2, 4), y, z, core)]
     for peer in peers:
         pl.semaphore_signal(barrier, inc=1, device_id=peer, device_id_type=pl.DeviceIdType.MESH)
 
     loads = [
-        pltpu.make_async_copy(ex_ref, stack.at[:ex], load.at[16]),
-        pltpu.make_async_copy(tgt_ref, stack.at[ex:], load.at[17]),
+        pltpu.make_async_copy(ex_ref, stack.at[:ex], load.at[8]),
+        pltpu.make_async_copy(tgt_ref, stack.at[ex:], load.at[9]),
     ]
-    for j in range(16):
-        owner = 2 * (j % 8) + (1 - core if j < 8 else core)
-        span = pl.ds(pl.multiple_of(owner * width, width), width)
+    for j in range(8):
+        span = pl.ds(2 * j * width, 2 * width)
         loads.append(pltpu.make_async_copy(proj_ref.at[:, span], pv.at[j], load.at[j]))
     for copy in loads:
         copy.start()
     loads[0].wait()
     loads[1].wait()
-    pl.semaphore_wait(barrier, len(peers))
-
-    e_pair = []
-    for j in range(16):
+    for j in range(8):
         loads[2 + j].wait()
         part = dot(stack[...], pv[j], 1, 0)
-        side = 0 if j < 8 else 1
-        ep[side, j % 8] = part[:ex]
-        tp[side, j % 8] = part[ex:]
-        if j < 8:
-            e_pair.append(push(ep.at[0, j], er.at[j], pair))
-    t_pair = push(tp.at[0], tr, pair)
-    landed(e_pair)
-    er[...] = er[...] + ep[1]
+        for c in range(2):
+            ep[c, j] = part[:ex, c * width : (c + 1) * width]
+            tp[c, j] = part[ex:, c * width : (c + 1) * width]
+    pl.semaphore_wait(barrier, len(peers))
+
+    e_pair = push(ep.at[1 - core], er, pair)
+    t_pair = push(tp.at[1 - core], tr, pair)
+    landed([e_pair])
+    er[...] = er[...] + ep[core]
     e_parts = chips(er, eg)
     landed([t_pair])
-    tr[...] = tr[...] + tp[1]
+    tr[...] = tr[...] + tp[core]
     landed(e_parts)
     mine = pl.ds(pl.multiple_of(d * ex, ex), ex)
     fall[mine, :] = summed(er, eg).astype(BF16)
@@ -211,7 +208,8 @@
     landed(chips(kr, kg))
     g[x, y, z, core] = summed(kr, kg)
 
-    run(ring(z, 8, lambda zz: g.at[x, y, zz, core], lambda zz: at(x, y, zz, core)))
+    own = g.at[x, y, z, core]
+    landed([push(own, own, at(x, y, (z + s) % 8, core)) for s in (4, 3, 5, 2, 6, 1, 7)])
     low, high = pl.ds(0, 4), pl.ds(4, 4)
     run(
         ring(x, 4, lambda xx: g.at[xx, y, low, core], lambda xx: at(xx, y, z, core)),
@@ -360,7 +358,7 @@
     vmem, anywhere = pl.BlockSpec(memory_space=pltpu.VMEM), pl.BlockSpec(memory_space=pl.ANY)
     scratch = [
         ((ex + tgt, depth), BF16),
-        ((16, depth, width), BF16),
+        ((8, depth, 2 * width), BF16),
         ((2, 8, ex, width), F32),
         ((8, ex, width), F32),
         ((7, ex, width), F32),
@@ -396,7 +394,7 @@
         out_specs=vmem,
         scratch_shapes=[pltpu.VMEM(*one) for one in scratch]
         + [
-            pltpu.SemaphoreType.DMA((18,)),
+            pltpu.SemaphoreType.DMA((10,)),
             pltpu.SemaphoreType.DMA((96,)),
             pltpu.SemaphoreType.DMA((96,)),
         ],

time: 165 us -> 150 us (0.909)
  Pallas kernels: 163 us -> 149 us
    pallas_call x1, Pallas kernels: 163 us -> 149 us  [on_device(): pl.pallas_call(functools.partial(scores_kernel, 1.0 / columns, math.sqrt(...]
where the time goes in v4:
time: 150 us
  Pallas kernels  149 us (99%)
  local copies, waits for them, and re-layouts  1.64 us (1%)
    pallas_call x1, Pallas kernels, on_device(): pl.pallas_call(functools.partial(scores_kernel, 1.0 / columns, math.sqrt(...  149 us

profile of v4, /device:TPU:1, one launch (start us, length us, event | category | flops | bytes accessed | tf_op | source)
XLA Modules:
  0.0 150.3 jit_solution(10259739745524141797)
XLA Ops:
  0.0 148.7 %shard_map.46 = f32[256,96]{1,0:T(8,128)} custom-call(bf16[96,1280]{1,0:T(8,128)(2,1)} %ex_ref.1, bf16[256,1280]{1,0:T(8,128)(2,1)} %tgt_ref.1, bf16[1280,4096]{1,0:T(8,128)(2,1)} %proj_ref.1, f32[1,96]{1,0:T(1,128)} %bitcast.1), custom_call_target="tpu_custom_call" | custom-call | tf_op jit(solution)/shard_map/pallas_call | solution.py:390
  148.7 1.6 %copy.5 = f32[256,96]{0,1:T(8,128)} copy(f32[256,96]{1,0:T(8,128)} %shard_map.46) | data formatting | bytes 196608 | tf_op jit(solution)/shard_map/pallas_call | solution.py:390

commit v5 on v4

--- a/solution.py
+++ b/solution.py
@@ -17,10 +17,18 @@
 
 
 def tile_place(t):
-    pair, offset = t // 13, t % 13
-    low = (offset + pair) // 12
-    row = pair + low * (11 - 2 * pair)
-    return row, row + offset - low * (12 - pair)
+    row, first = 0, 0
+    for q in range(1, 12):
+        past = (t + 80 - (12 * q - q * (q - 1) // 2)) // 80
+        row = row + past
+        first = first + past * (13 - q)
+    return row, row + t - first
+
+
+def tile_owner(t):
+    rank, slot = divmod(t, TILES)
+    half, rest = divmod(rank, 8)
+    return rest // 4, half * 4 + rest % 4, slot
 
 
 TILE_AT = {tile_place(t): t for t in range(78)}
@@ -41,11 +49,13 @@
 
 def factor_block(d_ref):
     rows = lax.broadcasted_iota(jnp.int32, (SUB, BLK), 0)
-    for s in range(BLK // SUB):
+    subs = BLK // SUB
+    own = d_ref[:SUB, :]
+    for s in range(subs):
         top = s * SUB
-        left = d_ref[top : top + SUB, :BLK]
-        right = d_ref[top : top + SUB, BLK:]
+        left, right = own[:, :BLK], own[:, BLK:]
         cols = [jnp.broadcast_to(left[:, top + j : top + j + 1], (SUB, BLK)) for j in range(SUB)]
+        lowers, scales, row_ls, row_rs = [], [], [], []
         for j in range(SUB):
             scale = lax.rsqrt(cols[j][j : j + 1, :])
             lower = jnp.where(rows > j, cols[j] * scale, 0.0)
@@ -55,14 +65,29 @@
             right = jnp.where(rows == j, row_r, right - lower * row_r)
             for k in range(j + 1, SUB):
                 cols[k] = cols[k] - lower * lower[k : k + 1, :]
+            lowers.append(lower)
+            scales.append(scale)
+            row_ls.append(row_l)
+            row_rs.append(row_r)
+        if s + 1 < subs:
+            nxt = d_ref[top + SUB : top + 2 * SUB, :]
+            next_l, next_r = nxt[:, :BLK], nxt[:, BLK:]
+            below = [jnp.broadcast_to(next_l[:, top + j : top + j + 1], (SUB, BLK)) for j in range(SUB)]
+            for j in range(SUB):
+                lower = below[j] * scales[j]
+                next_l = next_l - lower * row_ls[j]
+                next_r = next_r - lower * row_rs[j]
+                for k in range(j + 1, SUB):
+                    below[k] = below[k] - lower * lowers[j][k : k + 1, :]
+            own = jnp.concatenate([next_l, next_r], axis=1)
         both = jnp.concatenate([left, right], axis=1)
         d_ref[top : top + SUB, :] = both
-        if s + 1 < BLK // SUB:
+        if s + 2 < subs:
             hi, lo = split(both)
             lhs = jnp.concatenate([hi[:, :BLK], lo[:, :BLK], hi[:, :BLK]], axis=0)
             rhs = jnp.concatenate([hi, hi, lo], axis=0)
             update = dot(lhs, rhs, 0, 0)
-            d_ref[top + SUB :, :] = d_ref[top + SUB :, :] - update[top + SUB :, :]
+            d_ref[top + 2 * SUB :, :] = d_ref[top + 2 * SUB :, :] - update[top + 2 * SUB :, :]
 
 
 def scores_kernel(
@@ -88,6 +113,28 @@
         return (v + step + n) % n
 
     started = []
+    later = [None]
+
+    def act(copy, name):
+        if later[0] is None:
+            getattr(copy, name)()
+        else:
+            later[0].append((copy, name))
+
+    def recorded(gen):
+        parts = []
+        for live in [True] * 16:
+            later[0] = []
+            live = next(gen, "end") != "end"
+            parts.append(later[0])
+            if not live:
+                break
+        later[0] = None
+        return parts
+
+    def replay(part):
+        for copy, name in part:
+            getattr(copy, name)()
 
     def push(src, dst, device, now=True):
         i = len(started)
@@ -100,13 +147,13 @@
             device_id_type=pl.DeviceIdType.MESH,
         )
         if now:
-            copy.start()
+            act(copy, "start")
         started.append(copy)
         return copy
 
     def landed(copies):
         for copy in copies:
-            copy.wait_recv()
+            act(copy, "wait_recv")
 
     def ring(pos, n, block, device):
         got = []
@@ -169,16 +216,16 @@
     pl.semaphore_wait(barrier, len(peers))
 
     e_pair = push(ep.at[1 - core], er, pair)
-    t_pair = push(tp.at[1 - core], tr, pair)
     landed([e_pair])
     er[...] = er[...] + ep[core]
     e_parts = chips(er, eg)
+    t_pair = push(tp.at[1 - core], tr, pair)
     landed([t_pair])
     tr[...] = tr[...] + tp[core]
     landed(e_parts)
     mine = pl.ds(pl.multiple_of(d * ex, ex), ex)
     fall[mine, :] = summed(er, eg).astype(BF16)
-    t_parts = chips(tr, tg, (4, 2, 6))
+    t_parts = chips(tr, tg, (3, 5, 7))
 
     def feat_rows(hi, zz):
         return fall.at[pl.ds(pl.multiple_of((hi * 8 + zz) * ex, ex), ex), :]
@@ -198,7 +245,7 @@
     )
 
     for i in range(TILES):
-        r, c = tile_place((d * TILES + i) % 78)
+        r, c = tile_place(((z // 4 * 8 + x_hi * 4 + z % 4) * TILES + i) % 78)
         a = fall[pl.ds(pl.multiple_of(r * BLK, BLK), BLK), :]
         b = fall[pl.ds(pl.multiple_of(c * BLK, BLK), BLK), :]
         kp[:, :, i] = dot(a, b, 1, 1).reshape(8, 2, 8, BLK)
@@ -210,40 +257,62 @@
 
     own = g.at[x, y, z, core]
     landed([push(own, own, at(x, y, (z + s) % 8, core)) for s in (4, 3, 5, 2, 6, 1, 7)])
-    low, high = pl.ds(0, 4), pl.ds(4, 4)
-    run(
-        ring(x, 4, lambda xx: g.at[xx, y, low, core], lambda xx: at(xx, y, z, core)),
-        ring(y, 4, lambda yy: g.at[x, yy, high, core], lambda yy: at(x, yy, z, core)),
-    )
-    shared = []
-
-    def pass_on(ref):
-        shared.append(push(ref, ref, pair))
-
-    def last_y(yy):
-        return g.at[:, yy, low, core]
-
-    def last_x(xx):
-        return g.at[xx, :, high, core]
-
-    pass_on(last_y(y))
-    pass_on(last_x(x))
-    ring_y = ring(y, 4, last_y, lambda yy: at(x, yy, z, core))
-    ring_x = ring(x, 4, last_x, lambda xx: at(xx, y, z, core))
-    next(ring_y)
-    next(ring_x)
-    next(ring_y)
-    for sign in (1, -1):
-        pass_on(last_y(turn(y, sign, 4)))
-    next(ring_x)
-    for sign in (1, -1):
-        pass_on(last_x(turn(x, sign, 4)))
-    next(ring_y)
-    pass_on(last_y(turn(y, 2, 4)))
-    next(ring_x)
-    pass_on(last_x(turn(x, 2, 4)))
-    landed(shared)
-    t_parts += chips(tr, tg, (5, 3, 1, 7))
+
+    def gather(base):
+        one, two = pl.ds(base, 2), pl.ds(base + 2, 2)
+
+        def to_x(xx):
+            return at(xx, y, z, core)
+
+        def to_y(yy):
+            return at(x, yy, z, core)
+
+        def last_y(yy):
+            return g.at[:, yy, one, core]
+
+        def last_x(xx):
+            return g.at[xx, :, two, core]
+
+        shared = []
+
+        def pass_on(ref):
+            shared.append(push(ref, ref, pair))
+
+        first_x = ring(x, 4, lambda xx: g.at[xx, y, one, core], to_x)
+        first_y = ring(y, 4, lambda yy: g.at[x, yy, two, core], to_y)
+        next(first_x)
+        next(first_y)
+        yield
+        next(first_x)
+        next(first_y)
+        yield
+        next(first_x)
+        next(first_y)
+        ring_y, ring_x = ring(y, 4, last_y, to_y), ring(x, 4, last_x, to_x)
+        next(ring_y)
+        next(ring_x)
+        pass_on(last_y(y))
+        pass_on(last_x(x))
+        yield
+        next(ring_y)
+        next(ring_x)
+        for sign in (1, -1):
+            pass_on(last_y(turn(y, sign, 4)))
+            pass_on(last_x(turn(x, sign, 4)))
+        yield
+        next(ring_y)
+        pass_on(last_y(turn(y, 2, 4)))
+        next(ring_x)
+        pass_on(last_x(turn(x, 2, 4)))
+        landed(shared)
+        yield
+
+    for _ in gather(0):
+        pass
+    rest = recorded(gather(4))
+    replay(rest[0])
+    t_rest = chips(tr, tg, (4, 1, 2, 6), now=False)
+    t_parts += t_rest
 
     ident = (
         lax.broadcasted_iota(jnp.int32, (BLK, BLK), 0) == lax.broadcasted_iota(jnp.int32, (BLK, BLK), 1)
@@ -252,6 +321,17 @@
     c_parts = chips(cr, cg, now=False)
 
     def step(k, carry):
+        @pl.when(k == 1)
+        def _():
+            replay(rest[2])
+
+        @pl.when(k == 3)
+        def _():
+            replay(rest[4])
+            replay(rest[5])
+            for copy in t_rest:
+                copy.start()
+
         @pl.when(k == LATE_SUM)
         def _():
             landed(t_parts)
@@ -272,9 +352,9 @@
             @pl.when(k == kk)
             def _(kk=kk, first=first):
                 for cc in range(kk, blocks):
-                    owner, i = divmod(TILE_AT[kk, cc], TILES)
+                    o_hi, o_z, i = tile_owner(TILE_AT[kk, cc])
                     for q in range(BLK // 8):
-                        piece = g[owner // 8 * 2 + q // 2 % 2, q // 4, owner % 8, q % 2, i]
+                        piece = g[o_hi * 2 + q // 2 % 2, q // 4, o_z, q % 2, i]
                         row[8 * q : 8 * q + 8, cc * BLK : (cc + 1) * BLK] = piece * inverse
                 if kk:
                     upd = dot3(
@@ -290,6 +370,15 @@
 
         diag[:, BLK:] = ident
         factor_block(diag)
+
+        @pl.when(k == 0)
+        def _():
+            replay(rest[1])
+
+        @pl.when(k == 2)
+        def _():
+            replay(rest[3])
+
         inv_h, inv_l = split(diag[:, BLK:])
         place = pl.ds(pl.multiple_of(k * BLK, BLK), BLK)
         ih[place, :] = inv_h
@@ -395,8 +484,8 @@
         scratch_shapes=[pltpu.VMEM(*one) for one in scratch]
         + [
             pltpu.SemaphoreType.DMA((10,)),
-            pltpu.SemaphoreType.DMA((96,)),
-            pltpu.SemaphoreType.DMA((96,)),
+            pltpu.SemaphoreType.DMA((112,)),
+            pltpu.SemaphoreType.DMA((112,)),
         ],
         compiler_params=pltpu.CompilerParams(
             collective_id=0, has_side_effects=True, vmem_limit_bytes=63 * 2**20

time: 150 us -> 164 us (1.093)
  Pallas kernels: 149 us -> 162 us
    pallas_call x1, Pallas kernels: 149 us -> 162 us  [on_device(): pl.pallas_call(functools.partial(scores_kernel, 1.0 / columns, math.sqrt(...]
where the time goes in v5:
time: 164 us
  Pallas kernels  162 us (99%)
    pallas_call x1, Pallas kernels, on_device(): pl.pallas_call(functools.partial(scores_kernel, 1.0 / columns, math.sqrt(...  162 us

profile of v5, /device:TPU:1, one launch (start us, length us, event | category | flops | bytes accessed | tf_op | source)
XLA Modules:
  0.0 164.0 jit_solution(11036653062325127460)
XLA Ops:
  0.0 162.3 %shard_map.46 = f32[256,96]{1,0:T(8,128)} custom-call(bf16[96,1280]{1,0:T(8,128)(2,1)} %ex_ref.1, bf16[256,1280]{1,0:T(8,128)(2,1)} %tgt_ref.1, bf16[1280,4096]{1,0:T(8,128)(2,1)} %proj_ref.1, f32[1,96]{1,0:T(1,128)} %bitcast.1), custom_call_target="tpu_custom_call" | custom-call | tf_op jit(solution)/shard_map/pallas_call | solution.py:479
  162.3 1.6 copy.5

commit v6 on v5

--- a/solution.py
+++ b/solution.py
@@ -155,22 +155,6 @@
         for copy in copies:
             act(copy, "wait_recv")
 
-    def ring(pos, n, block, device):
-        got = []
-        for step in range(1, n // 2 + 1):
-            landed(got)
-            got = []
-            if step < n // 2:
-                for sign in (1, -1):
-                    ref = block(turn(pos, -sign * (step - 1), n))
-                    got.append(push(ref, ref, device(turn(pos, sign, n))))
-            else:
-                ref = block((pos - way * (step - 1) + n) % n)
-                got.append(push(ref, ref, device((pos + way + n) % n)))
-            yield
-        landed(got)
-        yield
-
     def run(*rings):
         live = list(rings)
         while live:
@@ -225,24 +209,37 @@
     landed(e_parts)
     mine = pl.ds(pl.multiple_of(d * ex, ex), ex)
     fall[mine, :] = summed(er, eg).astype(BF16)
-    t_parts = chips(tr, tg, (3, 5, 7))
 
     def feat_rows(hi, zz):
         return fall.at[pl.ds(pl.multiple_of((hi * 8 + zz) * ex, ex), ex), :]
 
     other = (x_hi + 1) % 2
 
-    def far_ring():
-        ref = feat_rows(x_hi, z)
-        copy = push(ref, ref, at(turn(x, 2, 4), y, z, core))
-        yield
-        copy.wait_recv()
-        yield from ring(z, 8, lambda zz: feat_rows(other, zz), lambda zz: at(x, y, zz, core))
-
-    run(
-        far_ring(),
-        ring(z, 8, lambda zz: feat_rows(x_hi, zz), lambda zz: at(x, y, zz, core)),
-    )
+    ref = feat_rows(x_hi, z)
+    far = push(ref, ref, at(turn(x, 2, 4), y, z, core))
+    t_parts = chips(tr, tg, (3, 5))
+
+    def along_z(hi):
+        own = feat_rows(hi, z)
+        near = [push(own, own, at(x, y, turn(z, step, 8), core)) for step in (2, -2, 1, -1)]
+        yield
+        landed(near)
+        back = [feat_rows(hi, turn(z, -2, 8)), feat_rows(hi, turn(z, 2, 8))]
+        away = feat_rows(hi, (z - 2 * way + 8) % 8)
+        near = [
+            push(away, away, at(x, y, (z + 2 * way + 8) % 8, core)),
+            push(back[0], back[0], at(x, y, turn(z, 1, 8), core)),
+            push(back[1], back[1], at(x, y, turn(z, -1, 8), core)),
+        ]
+        yield
+        landed(near)
+        yield
+
+    def far_z():
+        far.wait_recv()
+        yield from along_z(other)
+
+    run(along_z(x_hi), far_z())
 
     for i in range(TILES):
         r, c = tile_place(((z // 4 * 8 + x_hi * 4 + z % 4) * TILES + i) % 78)
@@ -278,32 +275,23 @@
         def pass_on(ref):
             shared.append(push(ref, ref, pair))
 
-        first_x = ring(x, 4, lambda xx: g.at[xx, y, one, core], to_x)
-        first_y = ring(y, 4, lambda yy: g.at[x, yy, two, core], to_y)
-        next(first_x)
-        next(first_y)
-        yield
-        next(first_x)
-        next(first_y)
-        yield
-        next(first_x)
-        next(first_y)
-        ring_y, ring_x = ring(y, 4, last_y, to_y), ring(x, 4, last_x, to_x)
-        next(ring_y)
-        next(ring_x)
+        def to_all(pos, block, device):
+            ref = block(pos)
+            return [push(ref, ref, device((pos + step) % 4)) for step in (2, 1, 3)]
+
+        first = to_all(x, lambda xx: g.at[xx, y, one, core], to_x)
+        first += to_all(y, lambda yy: g.at[x, yy, two, core], to_y)
+        yield
+        landed(first)
+        by_y, by_x = to_all(y, last_y, to_y), to_all(x, last_x, to_x)
         pass_on(last_y(y))
         pass_on(last_x(x))
         yield
-        next(ring_y)
-        next(ring_x)
-        for sign in (1, -1):
-            pass_on(last_y(turn(y, sign, 4)))
-            pass_on(last_x(turn(x, sign, 4)))
-        yield
-        next(ring_y)
-        pass_on(last_y(turn(y, 2, 4)))
-        next(ring_x)
-        pass_on(last_x(turn(x, 2, 4)))
+        for i, step in ((1, 3), (2, 1), (0, 2)):
+            landed([by_y[i]])
+            pass_on(last_y((y + step) % 4))
+            landed([by_x[i]])
+            pass_on(last_x((x + step) % 4))
         landed(shared)
         yield
 
@@ -311,26 +299,27 @@
         pass
     rest = recorded(gather(4))
     replay(rest[0])
-    t_rest = chips(tr, tg, (4, 1, 2, 6), now=False)
+    t_rest = chips(tr, tg, (4, 1, 7, 2, 6), now=False)
     t_parts += t_rest
 
     ident = (
         lax.broadcasted_iota(jnp.int32, (BLK, BLK), 0) == lax.broadcasted_iota(jnp.int32, (BLK, BLK), 1)
     ).astype(F32)
+
+    def late_tile(r, c):
+        return r == 3 and TILE_AT[r, c] >= 8 * TILES
+
+    def tile_rows(r, c, q):
+        o_hi, o_z, i = tile_owner(TILE_AT[r, c])
+        return g[o_hi * 2 + q // 2 % 2, q // 4, o_z, q % 2, i] * inverse
+
     c_pair = push(cp.at[:, 1 - core], cr, pair, False)
     c_parts = chips(cr, cg, now=False)
 
     def step(k, carry):
         @pl.when(k == 1)
         def _():
-            replay(rest[2])
-
-        @pl.when(k == 3)
-        def _():
-            replay(rest[4])
-            replay(rest[5])
-            for copy in t_rest:
-                copy.start()
+            replay(rest[1])
 
         @pl.when(k == LATE_SUM)
         def _():
@@ -352,10 +341,12 @@
             @pl.when(k == kk)
             def _(kk=kk, first=first):
                 for cc in range(kk, blocks):
-                    o_hi, o_z, i = tile_owner(TILE_AT[kk, cc])
+                    span = slice(cc * BLK, (cc + 1) * BLK)
+                    if late_tile(kk, cc):
+                        row[:, span] = jnp.zeros((BLK, BLK), F32)
+                        continue
                     for q in range(BLK // 8):
-                        piece = g[o_hi * 2 + q // 2 % 2, q // 4, o_z, q % 2, i]
-                        row[8 * q : 8 * q + 8, cc * BLK : (cc + 1) * BLK] = piece * inverse
+                        row[8 * q : 8 * q + 8, span] = tile_rows(kk, cc, q)
                 if kk:
                     upd = dot3(
                         uh[:first, first : first + BLK],
@@ -371,13 +362,11 @@
         diag[:, BLK:] = ident
         factor_block(diag)
 
-        @pl.when(k == 0)
+        @pl.when(k == 3)
         def _():
-            replay(rest[1])
-
-        @pl.when(k == 2)
-        def _():
-            replay(rest[3])
+            replay(rest[2])
+            for copy in t_rest:
+                copy.start()
 
         inv_h, inv_l = split(diag[:, BLK:])
         place = pl.ds(pl.multiple_of(k * BLK, BLK), BLK)
@@ -387,7 +376,12 @@
             last = (kk + 1) * BLK
 
             @pl.when(k == kk)
-            def _(last=last):
+            def _(kk=kk, last=last):
+                for cc in range(kk, blocks):
+                    span = slice(cc * BLK, (cc + 1) * BLK)
+                    if late_tile(kk, cc):
+                        for q in range(BLK // 8):
+                            row[8 * q : 8 * q + 8, span] += tile_rows(kk, cc, q)
                 a_h, a_l = split(row[:, last:])
                 u_h, u_l = split(dot3(inv_h, inv_l, a_h, a_l, 1, 0))
                 uh[last - BLK : last, last:] = u_h

time: 164 us -> 138 us (0.84)
  Pallas kernels: 162 us -> 136 us
    pallas_call x1, Pallas kernels: 162 us -> 136 us  [on_device(): pl.pallas_call(functools.partial(scores_kernel, 1.0 / columns, math.sqrt(...]
where the time goes in v6:
time: 138 us
  Pallas kernels  136 us (99%)
  local copies, waits for them, and re-layouts  1.64 us (1%)
    pallas_call x1, Pallas kernels, on_device(): pl.pallas_call(functools.partial(scores_kernel, 1.0 / columns, math.sqrt(...  136 us

profile of v6, /device:TPU:1, one launch (start us, length us, event | category | flops | bytes accessed | tf_op | source)
XLA Modules:
  0.0 138.0 jit_solution(10163657883004228942)
XLA Ops:
  0.0 136.4 %shard_map.46 = f32[256,96]{1,0:T(8,128)} custom-call(bf16[96,1280]{1,0:T(8,128)(2,1)} %ex_ref.1, bf16[256,1280]{1,0:T(8,128)(2,1)} %tgt_ref.1, bf16[1280,4096]{1,0:T(8,128)(2,1)} %proj_ref.1, f32[1,96]{1,0:T(1,128)} %bitcast.1), custom_call_target="tpu_custom_call" | custom-call | tf_op jit(solution)/shard_map/pallas_call | solution.py:473
  136.4 1.6 %copy.5 = f32[256,96]{0,1:T(8,128)} copy(f32[256,96]{1,0:T(8,128)} %shard_map.46) | data formatting | bytes 196608 | tf_op jit(solution)/shard_map/pallas_call | solution.py:473

commit v7 on v6

--- a/solution.py
+++ b/solution.py
@@ -12,7 +12,7 @@
 BLK = 128
 SUB = 16
 TILES = 5
-LATE_SUM = 8
+LATE_SUM = 7
 F32, BF16 = jnp.float32, jnp.bfloat16
 
 
@@ -295,12 +295,14 @@
         landed(shared)
         yield
 
-    for _ in gather(0):
-        pass
+    upper = gather(0)
+    next(upper)
     rest = recorded(gather(4))
     replay(rest[0])
-    t_rest = chips(tr, tg, (4, 1, 7, 2, 6), now=False)
-    t_parts += t_rest
+    for _ in upper:
+        pass
+    replay(rest[1])
+    t_parts += chips(tr, tg, (4, 1, 7, 2, 6))
 
     ident = (
         lax.broadcasted_iota(jnp.int32, (BLK, BLK), 0) == lax.broadcasted_iota(jnp.int32, (BLK, BLK), 1)
@@ -317,10 +319,6 @@
     c_parts = chips(cr, cg, now=False)
 
     def step(k, carry):
-        @pl.when(k == 1)
-        def _():
-            replay(rest[1])
-
         @pl.when(k == LATE_SUM)
         def _():
             landed(t_parts)
@@ -365,8 +363,6 @@
         @pl.when(k == 3)
         def _():
             replay(rest[2])
-            for copy in t_rest:
-                copy.start()
 
         inv_h, inv_l = split(diag[:, BLK:])
         place = pl.ds(pl.multiple_of(k * BLK, BLK), BLK)

time: 138 us -> 134 us (0.971)
  Pallas kernels: 136 us -> 132 us
    pallas_call x1, Pallas kernels: 136 us -> 132 us  [on_device(): pl.pallas_call(functools.partial(scores_kernel, 1.0 / columns, math.sqrt(...]
where the time goes in v7:
time: 134 us
  Pallas kernels  132 us (99%)
  local copies, waits for them, and re-layouts  1.64 us (1%)
    pallas_call x1, Pallas kernels, on_device(): pl.pallas_call(functools.partial(scores_kernel, 1.0 / columns, math.sqrt(...  132 us

profile of v7, /device:TPU:1, one launch (start us, length us, event | category | flops | bytes accessed | tf_op | source)
XLA Modules:
  0.0 133.8 jit_solution(13693247356680810865)
XLA Ops:
  0.0 132.1 %shard_map.46 = f32[256,96]{1,0:T(8,128)} custom-call(bf16[96,1280]{1,0:T(8,128)(2,1)} %ex_ref.1, bf16[256,1280]{1,0:T(8,128)(2,1)} %tgt_ref.1, bf16[1280,4096]{1,0:T(8,128)(2,1)} %proj_ref.1, f32[1,96]{1,0:T(1,128)} %bitcast.1), custom_call_target="tpu_custom_call" | custom-call | tf_op jit(solution)/shard_map/pallas_call | solution.py:469
  132.2 1.6 %copy.5 = f32[256,96]{0,1:T(8,128)} copy(f32[256,96]{1,0:T(8,128)} %shard_map.46) | data formatting | bytes 196608 | tf_op jit(solution)/shard_map/pallas_call | solution.py:469
